TPU v7x, 64 devices: a 2x2x8 block of a 4x4x8 slice. The times are simulated.
64 devices in a mesh: dp: 4 (over x, y), sp: 16 (over z, core).
Axes of the slice: x: 2, y: 2, z: 8, core: 2. Of those that a mesh axis runs over, the one named last changes fastest.
The devices are a block of a 4x4x8 slice.
Arguments:
- prompt: bfloat16 [4, 1024, 4096], P('dp', 'sp'), parts along dimension 0
- w_q: bfloat16 [4096, 4096], replicated
- w_k: bfloat16 [4096, 4096], replicated
- w_v: bfloat16 [4096, 4096], replicated
- w_o: bfloat16 [4096, 4096], replicated
- q_norm_w: float32 [4096], replicated
- k_norm_w: float32 [4096], replicated
- post_norm_w: float32 [4096], replicated
- new_token: bfloat16 [4, 4096], P('dp'), parts along dimension 0
Outputs:
- output 1: bfloat16 [4, 1024, 4096], P('dp', 'sp'), parts along dimension 0
- output 2: bfloat16 [4, 1025, 32, 128], P('dp', None, 'sp'), parts along dimension 0
- output 3: bfloat16 [4, 1025, 32, 128], P('dp', None, 'sp'), parts along dimension 0
- output 4: bfloat16 [4, 4096], P('dp'), parts along dimension 0
There are 4 independent parts. A program takes and returns all parts, laid end to end along the dimension named above; an argument that names none is the same for every part.
All inputs are finite; a program needn't handle non-finite values.
Results may differ from a plain program's by a relative error of at most 0.00684954.
Values are sent between devices in bfloat16 or wider.
A program may use at most 768 MiB of HBM per device.

v0:
```python
import jax
import jax.numpy as jnp
from jax import lax
from jax.sharding import PartitionSpec as P

HEAD_DIM = 128
ROPE_THETA = 500000.0
NORM_EPS = 1e-6


def rms_norm(values, weight):
    return values * lax.rsqrt(jnp.mean(values * values, axis=-1, keepdims=True) + NORM_EPS) * weight


def rope_tables(positions):
    inv_freq = ROPE_THETA ** (-jnp.arange(0, HEAD_DIM, 2).astype(jnp.float32) / HEAD_DIM)
    angles = positions.astype(jnp.float32)[:, None] * inv_freq[None, :]
    angles = jnp.concatenate([angles, angles], axis=-1)
    return jnp.cos(angles), jnp.sin(angles)


def apply_rope(values, cos_t, sin_t):
    half_dim = HEAD_DIM // 2
    rotated = jnp.concatenate([-values[..., half_dim:], values[..., :half_dim]], axis=-1)
    return values * cos_t[:, None, :] + rotated * sin_t[:, None, :]


def project_heads(x_rows, w_mat, norm_w, cos_t, sin_t):
    normed = rms_norm(jnp.dot(x_rows, w_mat, preferred_element_type=jnp.float32), norm_w)
    return apply_rope(normed.reshape(x_rows.shape[:-1] + (-1, HEAD_DIM)), cos_t, sin_t).astype(jnp.bfloat16)


def causal_attention(q_loc, k_all, v_all, q_start):
    n_batch, tok_len, n_heads, head_dim = q_loc.shape
    block_rows = min(tok_len, 128)
    key_pos = jnp.arange(k_all.shape[1])
    score_scale = head_dim ** -0.5

    def one_block(block_idx):
        q_blk = lax.dynamic_slice_in_dim(q_loc, block_idx * block_rows, block_rows, axis=1)
        q_pos = q_start + block_idx * block_rows + jnp.arange(block_rows)
        scores = jnp.einsum("bqhd,bkhd->bhqk", q_blk, k_all, preferred_element_type=jnp.float32) * score_scale
        scores = jnp.where((q_pos[:, None] >= key_pos[None, :])[None, None], scores, -1e30)
        attn_p = jax.nn.softmax(scores, axis=-1).astype(jnp.bfloat16)
        return jnp.einsum("bhqk,bkhd->bqhd", attn_p, v_all, preferred_element_type=jnp.float32).astype(jnp.bfloat16)

    blocks = lax.map(one_block, jnp.arange(tok_len // block_rows))
    return jnp.moveaxis(blocks, 0, 1).reshape(n_batch, tok_len, n_heads * head_dim)


def solution(mesh):
    group_n = mesh.shape["sp"]

    def device_step(prompt_blk, w_q, w_k, w_v, w_o, q_norm_w, k_norm_w, post_norm_w, new_rows):
        n_batch, tok_len, full_width = prompt_blk.shape
        n_heads = full_width // HEAD_DIM
        heads_loc = n_heads // group_n
        cols_loc = heads_loc * HEAD_DIM
        my_index = lax.axis_index("sp")
        q_start = my_index * tok_len
        cos_p, sin_p = rope_tables(q_start + jnp.arange(tok_len))
        q_loc = project_heads(prompt_blk, w_q, q_norm_w, cos_p, sin_p)
        k_loc = project_heads(prompt_blk, w_k, k_norm_w, cos_p, sin_p)
        v_loc = jnp.dot(prompt_blk, w_v, preferred_element_type=jnp.float32).astype(jnp.bfloat16).reshape(n_batch, tok_len, n_heads, HEAD_DIM)
        k_all = lax.all_gather(k_loc, "sp", axis=1, tiled=True)
        v_all = lax.all_gather(v_loc, "sp", axis=1, tiled=True)
        attn_out = causal_attention(q_loc, k_all, v_all, q_start)
        proj_pre = jnp.dot(attn_out, w_o, preferred_element_type=jnp.float32)
        out_p = (prompt_blk.astype(jnp.float32) + rms_norm(proj_pre, post_norm_w)).astype(jnp.bfloat16)
        k_mine = lax.dynamic_slice_in_dim(k_all, my_index * heads_loc, heads_loc, axis=2)
        v_mine = lax.dynamic_slice_in_dim(v_all, my_index * heads_loc, heads_loc, axis=2)
        col_start = my_index * cols_loc
        q_raw = jnp.dot(new_rows, lax.dynamic_slice_in_dim(w_q, col_start, cols_loc, axis=1), preferred_element_type=jnp.float32)
        k_raw = jnp.dot(new_rows, lax.dynamic_slice_in_dim(w_k, col_start, cols_loc, axis=1), preferred_element_type=jnp.float32)
        v_new = jnp.dot(new_rows, lax.dynamic_slice_in_dim(w_v, col_start, cols_loc, axis=1), preferred_element_type=jnp.float32).astype(jnp.bfloat16).reshape(n_batch, heads_loc, HEAD_DIM)
        sq_sums = jnp.stack([jnp.sum(q_raw * q_raw, axis=-1), jnp.sum(k_raw * k_raw, axis=-1)], axis=-1)
        sq_total = lax.psum(sq_sums, "sp")
        cos_d, sin_d = rope_tables(jnp.full((1,), tok_len * group_n))
        q_scaled = q_raw * lax.rsqrt(sq_total[:, 0:1] / full_width + NORM_EPS) * lax.dynamic_slice_in_dim(q_norm_w, col_start, cols_loc)
        k_scaled = k_raw * lax.rsqrt(sq_total[:, 1:2] / full_width + NORM_EPS) * lax.dynamic_slice_in_dim(k_norm_w, col_start, cols_loc)
        q_new = apply_rope(q_scaled.reshape(n_batch, heads_loc, HEAD_DIM), cos_d, sin_d).astype(jnp.bfloat16)
        k_new = apply_rope(k_scaled.reshape(n_batch, heads_loc, HEAD_DIM), cos_d, sin_d).astype(jnp.bfloat16)
        k_cache = jnp.concatenate([k_mine, k_new[:, None]], axis=1)
        v_cache = jnp.concatenate([v_mine, v_new[:, None]], axis=1)
        scores = jnp.einsum("bhd,bkhd->bhk", q_new, k_cache, preferred_element_type=jnp.float32) * HEAD_DIM ** -0.5
        attn_d = jax.nn.softmax(scores, axis=-1).astype(jnp.bfloat16)
        o_new = jnp.einsum("bhk,bkhd->bhd", attn_d, v_cache, preferred_element_type=jnp.float32).astype(jnp.bfloat16).reshape(n_batch, cols_loc)
        part_proj = jnp.dot(o_new, lax.dynamic_slice_in_dim(w_o, col_start, cols_loc, axis=0), preferred_element_type=jnp.float32).astype(jnp.bfloat16)
        all_parts = lax.all_gather(part_proj, "sp")
        proj_new = jnp.sum(all_parts.astype(jnp.float32), axis=0)
        out_d = (new_rows.astype(jnp.float32) + rms_norm(proj_new, post_norm_w)).astype(jnp.bfloat16)
        return out_p, k_cache, v_cache, out_d

    replicated = P()
    return jax.shard_map(
        device_step, mesh=mesh,
        in_specs=(P("dp", "sp", None), replicated, replicated, replicated, replicated, replicated, replicated, replicated, P("dp", None)),
        out_specs=(P("dp", "sp", None), P("dp", None, "sp", None), P("dp", None, "sp", None), P("dp", None)),
        check_vma=False)
```

profile of v0, /device:TPU:21, one launch (start us, length us, event | category | flops | bytes accessed | tf_op | source)
XLA Modules:
  0.0 211.4 jit_solution(11500343467068464873)
XLA Ops:
  7.6 13.9 %multiply_reduce_fusion.1 = (f32[64]{0:T(128)S(1)}, f32[64,4096]{1,0:T(8,128)S(1)}) fusion(bf16[4096,4096]{1,0:T(8,128)(2,1)} %param.11, bf16[1,64,4096]{2,1,0:T(8,128)(2,1)} %param.9), kind=kOutput, calls=%fused_computation.40 | convolution fusion | flops 2148007936 | bytes 35127552 | tf_op jit(solution)/shard_map/dot_general | solution.py:29
  21.9 0.6 copy.54
  22.5 0.4 slice_negate_fusion
  22.9 1.6 fusion.28
  24.6 13.6 %fusion.24 = bf16[8,8,32,128]{3,1,2,0:T(8,128)(2,1)S(1)} fusion(bf16[4096,4096]{1,0:T(8,128)(2,1)} %param.12, bf16[1,64,4096]{2,1,0:T(8,128)(2,1)S(1)} %copy-done), kind=kOutput, calls=%fused_computation.24 | convolution fusion | flops 2147745792 | bytes 34603008 | tf_op jit(solution)/shard_map/dot_general | solution.py:64
  38.3 1.0 copy.50
  39.4 2.0 fusion.14
  41.4 0.6 multiply_reduce_fusion.5
  42.0 2.0 fusion.16
  44.0 0.6 multiply_reduce_fusion.4
  44.6 1.4 pad_maximum_fusion.3
  45.9 30.7 %psum.7 = f32[1,2]{1,0:T(1,128)S(1)} all-reduce(f32[1,2]{1,0:T(1,128)S(1)} %pad_maximum_fusion.3), channel_id=1, replica_groups=mesh['dp'=4,'sp'=16] {'sp'}, use_global_device_ids=true, to_apply=%region_7.8 | all-reduce | flops 2 | bytes 16 | tf_op jit(solution)/shard_map/psum | solution.py:77
  76.7 0.6 fusion.75
  78.6 2.0 fusion.12
  80.6 13.7 %multiply_reduce_fusion.2 = (f32[64]{0:T(128)S(1)}, f32[64,4096]{1,0:T(8,128)S(1)}) fusion(bf16[4096,4096]{1,0:T(8,128)(2,1)} %param.10, bf16[1,64,4096]{2,1,0:T(8,128)(2,1)S(1)} %copy-done), kind=kOutput, calls=%fused_computation.42 | convolution fusion | flops 2148007936 | bytes 35127552 | tf_op jit(solution)/shard_map/dot_general | solution.py:29
  95.4 0.7 iota_compare_fusion
  96.5 2.3 %copy_bitcast_fusion = (f32[64,32,64]{2,0,1:T(8,128)S(1)}, f32[64,32,64]{2,0,1:T(8,128)}) fusion(f32[1,64,32,64]{3,2,1,0:T(8,128)S(1)} %get-tuple-element.44, f32[1,64,32,64]{3,2,1,0:T(8,128)S(1)} %get-tuple-element.43), kind=kLoop, calls=%fused_computation.33 | loop fusion | flops 131072 | bytes 2097152 | tf_op jit(solution)/shard_map/concatenate | solution.py:24
  98.8 37.0 %all-gather.4.cloned.1.call-done = bf16[1,1024,32,128]{3,1,2,0:T(8,128)(2,1)} async-done(((bf16[1,64,32,128]{3,1,2,0:T(8,128)(2,1)}), bf16[1,1024,32,128]{3,1,2,0:T(8,128)(2,1)}) %all-gather.4.cloned.1.call-update) | async-done | bytes 8388624 | tf_op jit(solution)/shard_map/all_gather | solution.py:66
  135.8 1.3 constant_dynamic-slice_fusion
  137.8 0.9 pad_maximum_fusion.1
  138.9 2.0 fusion.10
  140.9 16.0 %all-gather = bf16[65536]{0:T(1024)(128)(2,1)S(1)} all-gather(bf16[4096]{0:T(1024)(128)(2,1)S(1)} %convert_element_type.131), channel_id=2, replica_groups=mesh['dp'=4,'sp'=16] {'sp'}, dimensions={0}, use_global_device_ids=true | all-gather | bytes 139264 | tf_op jit(solution)/shard_map/all_gather | solution.py:89
  157.0 0.6 multiply_reduce_fusion.3
  158.3 0.7 multiply_multiply_fusion.1
  159.0 1.3 add_convert_fusion
  160.4 6.8 %fusion.1 = f32[32,64,1024]{2,1,0:T(8,128)S(1)} fusion(bf16[1,1024,32,128]{3,1,2,0:T(8,128)(2,1)} %all-gather.6.cloned.1.call-done, f32[8,32,8,128]{3,2,1,0:T(8,128)S(1)} %get-tuple-element.42, f32[64,32,64]{2,0,1:T(8,128)S(1)} %get-tuple-element.65, f32[64,32,64]{2,0,1:T(8,128)} %get-tuple-element.66, f32[64,128]{1,0:T(8,128)} %copy-done.3, ...), kind=kOutput, calls=%fused_computation.1 | convolution fusion | flops 538181632 | bytes 18939904 | tf_op jit(solution)/shard_map/while/body/eval_jaxpr/bqhd,bkhd->bhqk/dot_general | solution.py:42
  167.2 5.7 %fusion.76 = (f32[32,64]{1,0:T(8,128)S(1)}, f32[32,64,1024]{2,1,0:T(8,128)}) fusion(f32[32,64,1024]{2,1,0:T(8,128)S(1)} %fusion.1, pred[64,1024]{1,0:T(8,128)(4,1)S(1)} %copy-done.6), kind=kOutput, calls=%fused_computation.120 | output fusion | flops 12583935 | bytes 16850944 | tf_op jit(solution)/shard_map/while/body/eval_jaxpr/sub | solution.py:44
  172.9 7.4 %fusion.21 = bf16[1,64,32,128]{3,1,2,0:T(8,128)(2,1)S(1)} fusion(bf16[1,1024,32,128]{3,1,2,0:T(8,128)(2,1)} %all-gather.4.cloned.1.call-done, f32[32,64,1024]{2,1,0:T(8,128)} %get-tuple-element.62, f32[32,64]{1,0:T(8,128)S(1)} %get-tuple-element.61), kind=kOutput, calls=%fused_computation.23 | convolution fusion | flops 541327360 | bytes 17309696 | tf_op jit(solution)/shard_map/while/body/eval_jaxpr/bhqk,bkhd->bqhd/dot_general | solution.py:45
  180.7 13.8 %multiply_reduce_fusion = (f32[64]{0:T(128)S(1)}, f32[64,4096]{1,0:T(8,128)S(1)}) fusion(bf16[4096,4096]{1,0:T(8,128)(2,1)} %param.13, bf16[8,8,32,128]{3,2,1,0:T(8,128)(2,1)S(1)} %bitcast.129), kind=kOutput, calls=%fused_computation.38 | convolution fusion | flops 2148007936 | bytes 35127552 | tf_op jit(solution)/shard_map/dot_general | solution.py:68
  194.5 4.5 %copy.61 = bf16[1,1025,2,128]{3,2,1,0:T(2,128)(2,1)} copy(bf16[1,1025,2,128]{3,1,2,0:T(8,128)(2,1)S(1)} %pad_maximum_fusion) | data formatting | bytes 1049600
  199.0 4.5 %copy.62 = bf16[1,1025,2,128]{3,2,1,0:T(2,128)(2,1)} copy(bf16[1,1025,2,128]{3,1,2,0:T(8,128)(2,1)S(1)} %copy-done.1) | data formatting | bytes 1049600
  203.5 1.0 fusion.30
  (59 shorter events, 3.7 us)
Async XLA Ops:
  7.2 91.6 %all-gather.6.cloned.1.call-start = ((), (), s32[]{:S(2)}) async-start(), calls=%async_computation.1 | async-start | bytes 8912896 | tf_op jit(solution)/shard_map/all_gather | solution.py:65
  7.6 15.3 %copy-start.2 = (f32[64,128]{1,0:T(8,128)}, f32[64,128]{1,0:T(8,128)S(1)}, u32[]{:S(2)}) copy-start(f32[64,128]{1,0:T(8,128)S(1)} %get-tuple-element.47) | copy-start | bytes 98308
  7.6 15.3 %copy-start.3 = (f32[64,128]{1,0:T(8,128)}, f32[64,128]{1,0:T(8,128)S(1)}, u32[]{:S(2)}) copy-start(f32[64,128]{1,0:T(8,128)S(1)} %get-tuple-element.48) | copy-start | bytes 98308
  7.6 13.9 %copy-start.8 = (f32[4096]{0:T(1024)S(1)}, f32[4096]{0:T(1024)}, u32[]{:S(2)}) copy-start(f32[4096]{0:T(1024)} %param.15) | copy-start | bytes 49156
  21.5 3.1 %copy-start = (bf16[1,64,4096]{2,1,0:T(8,128)(2,1)S(1)}, bf16[1,64,4096]{2,1,0:T(8,128)(2,1)}, u32[]{:S(2)}) copy-start(bf16[1,64,4096]{2,1,0:T(8,128)(2,1)} %param.9) | copy-start | bytes 1572868
  24.5 14.9 %copy-start.4 = (bf16[1,4096]{1,0:T(2,128)(2,1)S(1)}, bf16[1,4096]{1,0:T(2,128)(2,1)}, u32[]{:S(2)}) copy-start(bf16[1,4096]{1,0:T(2,128)(2,1)} %param.17) | copy-start | bytes 24580
  24.5 111.3 %all-gather.4.cloned.1.call-start = ((), (), s32[]{:S(2)}) async-start(), calls=%async_computation | async-start | bytes 8912896 | tf_op jit(solution)/shard_map/all_gather | solution.py:66
  80.6 13.7 %copy-start.7 = (f32[4096]{0:T(1024)S(1)}, f32[4096]{0:T(1024)}, u32[]{:S(2)}) copy-start(f32[4096]{0:T(1024)} %param.14) | copy-start | bytes 49156
  160.4 6.8 %copy-start.6 = (pred[64,1024]{1,0:T(8,128)(4,1)S(1)}, pred[64,1024]{1,0:T(8,128)(4,1)}, u32[]{:S(2)}) copy-start(pred[64,1024]{1,0:T(8,128)(4,1)} %iota_compare_fusion) | copy-start | bytes 196612
  180.7 18.4 %copy-start.1 = (bf16[1,1025,2,128]{3,1,2,0:T(8,128)(2,1)S(1)}, bf16[1,1025,2,128]{3,1,2,0:T(8,128)(2,1)}, u32[]{:S(2)}) copy-start(bf16[1,1025,2,128]{3,1,2,0:T(8,128)(2,1)} %pad_maximum_fusion.1) | copy-start | bytes 1574404
  180.7 22.9 %copy-start.5 = (f32[4096]{0:T(1024)S(1)}, f32[4096]{0:T(1024)}, u32[]{:S(2)}) copy-start(f32[4096]{0:T(1024)} %param.16) | copy-start | bytes 49156
Sparse Core Ops, SparseCore 0:
  24.6 57.8 all-gather.5
  84.8 51.0 all-gather.3
where the time goes:
time: 212 us; the launch traced here: 211 us
  matrix products  77.5 us (37%)
  blocking collectives  46.7 us (22%)
  waiting for transfers between devices  37.1 us (18%)
  other arithmetic  19.6 us (9%)
  between operations  16.5 us (8%)
  local copies, waits for them, and re-layouts  13.8 us (7%)
    all_gather x1, waiting for transfers between devices, device_step(): v_all = lax.all_gather(v_loc, 'sp', axis=1, tiled=True)  37 us
    psum x1, blocking collectives, device_step(): sq_total = lax.psum(sq_sums, 'sp')  30.7 us
    dot_general x2, matrix products, project_heads(): jnp.dot(x_rows, w_mat, preferred_element_type=jnp.float32)  27.6 us
    all_gather x1, blocking collectives, device_step(): all_parts = lax.all_gather(part_proj, 'sp')  16 us
    dot_general x1, matrix products, device_step(): proj_pre = jnp.dot(attn_out, w_o, preferred_element_type=jnp.float32)  13.8 us
    dot_general x1, matrix products, device_step(): jnp.dot(prompt_blk, w_v, preferred_element_type=jnp.float32)  13.6 us
    unnamed x23, local copies, waits for them, and re-layouts  9.53 us
    dot_general x1, matrix products, one_block(): jnp.einsum('bhqk,bkhd->bqhd', attn_p, v_all, preferred_element_type=jnp.f...  7.37 us
  transfers between devices with their start and end apart: 2, of which 1 were waited for; matrix products, arithmetic and copies ran while one was open for 20% of the time, Pallas kernels for 0%

commit v1 on v0

v1 whole, which is shorter than its diff:
```python
import functools
import math

import jax
import jax.numpy as jnp
import numpy as np
from jax import lax
from jax.experimental import pallas as pl
from jax.experimental.pallas import tpu as pltpu
from jax.sharding import PartitionSpec as P

HEAD_DIM = 128
ROPE_THETA = 500000.0
NORM_EPS = 1e-6
PAD = 16
MASKED = -1e30
F32 = jnp.float32
BF16 = jnp.bfloat16
MESH = pl.DeviceIdType.MESH


def rope_table(seq_len):
    half = HEAD_DIM // 2
    inv_freq = np.power(np.float32(ROPE_THETA), -np.arange(0, HEAD_DIM, 2).astype(np.float32) / np.float32(HEAD_DIM)).astype(np.float32)
    pos = np.minimum(np.arange(seq_len + PAD), seq_len).astype(np.float32)
    angles = (pos[:, None] * inv_freq[None, :half]).astype(np.float32)
    return np.concatenate([np.cos(angles), np.sin(angles)], axis=-1).astype(np.float32)


def kernel(n_dev, x_hbm, new_ref, wq, wk, wv, wo, qg_ref, kg_ref, pg_ref, tab_hbm,
           outp_ref, kc_hbm, vc_hbm, outd_ref,
           xs, pool, tab, raw, ssq, ssq_in, send, recv, new, s_ref, p_ref, osend, orecv, dsend, dsum, acc, stage, cache,
           xsem, wsem, wosem, tabsem, xs_s, xs_r, ss_s, ss_r, a_s, a_r, d_s, d_r, o_s, o_r, csem):
    tok = x_hbm.shape[0]
    width = x_hbm.shape[1]
    rows = 2 * tok
    n_chip = n_dev // 2
    half_chip = n_chip // 2
    cols = width // n_dev
    heads = cols // HEAD_DIM
    seq = tok * n_dev
    n_step = n_chip // 2
    n_wo = pool.shape[0]
    wide = 2 * cols

    me = lax.axis_index("sp")
    chip = lax.div(me, 2)
    core = lax.rem(me, 2)
    sibling = 2 * chip + (1 - core)

    def offset_of(idx):
        odd = lax.rem(idx, 2)
        return lax.rem(half_chip + odd + (2 * odd - 1) * lax.div(idx, 2), n_chip)

    def group_col(idx):
        dest = lax.rem(chip + offset_of(idx), n_chip)
        return pl.multiple_of((2 * dest + core) * cols, cols)

    def w_copy(w_ref, s, half):
        return pltpu.make_async_copy(
            w_ref.at[:, pl.ds(group_col(2 * s + half), cols)], pool.at[s, :, pl.ds(half * cols, cols)], wsem.at[s, half])

    def wo_copy(j):
        return pltpu.make_async_copy(wo.at[:, pl.ds(pl.multiple_of(j * wide, wide), wide)], pool.at[j], wosem.at[j])

    my_rows = pl.ds(pl.multiple_of(core * tok, tok), tok)
    x_copy = pltpu.make_async_copy(x_hbm, xs.at[my_rows], xsem)
    x_copy.start()
    for s in range(n_step):
        w_copy(wv, s, 0).start()
        w_copy(wv, s, 1).start()
    tab_a = pltpu.make_async_copy(tab_hbm.at[pl.ds(pl.multiple_of(chip * rows, rows), rows)], tab.at[pl.ds(0, rows)], tabsem.at[0])
    tab_b = pltpu.make_async_copy(tab_hbm.at[pl.ds(seq, PAD)], tab.at[pl.ds(rows, PAD)], tabsem.at[1])
    tab_a.start()
    tab_b.start()

    barrier = pltpu.get_barrier_semaphore()
    for off in range(1, n_dev):
        pl.semaphore_signal(barrier, inc=1, device_id={"sp": lax.rem(me + off, n_dev)}, device_id_type=MESH)
    xs[pl.ds(rows, PAD), :] = jnp.broadcast_to(new_ref[...], (PAD, width))
    x_copy.wait()
    pl.semaphore_wait(barrier, n_dev - 1)

    x_send = pltpu.make_async_remote_copy(
        src_ref=xs.at[my_rows], dst_ref=xs.at[my_rows], send_sem=xs_s, recv_sem=xs_r, device_id={"sp": sibling}, device_id_type=MESH)
    x_send.start()
    x_send.wait_recv()

    own_rows = pl.ds(pl.multiple_of(chip * rows, rows), rows)

    def exchange(t, idx):
        dest = lax.rem(chip + offset_of(idx), n_chip)
        return pltpu.make_async_remote_copy(
            src_ref=send.at[t, idx], dst_ref=recv.at[t, own_rows], send_sem=a_s.at[t, idx], recv_sem=a_r.at[t, idx],
            device_id={"sp": 2 * dest + core}, device_id_type=MESH)

    def emit(t, idx, block):
        @pl.when(idx < n_chip - 1)
        def _():
            send[t, idx] = block[:rows]
            exchange(t, idx).start()

        @pl.when(idx == n_chip - 1)
        def _():
            recv[t, own_rows, :] = block[:rows]
            new[t] = block[rows:]

    def project(s):
        w_copy(wv, s, 0).wait()
        w_copy(wv, s, 1).wait()
        return jnp.dot(xs[...], pool[s], preferred_element_type=F32)

    def v_step(s, carry):
        res = project(s)
        w_copy(wk, s, 0).start()
        w_copy(wk, s, 1).start()
        for half in range(2):
            emit(2, 2 * s + half, res[:, half * cols:(half + 1) * cols].astype(BF16))
        return carry

    lax.fori_loop(0, n_step, v_step, 0)
    tab_a.wait()
    tab_b.wait()

    lane = lax.broadcasted_iota(jnp.int32, (rows + PAD, HEAD_DIM), 1)
    first = lane < HEAD_DIM // 2

    def raw_step(t, s):
        res = project(s)
        sq = jnp.zeros((rows + PAD, HEAD_DIM), F32)
        for half in range(2):
            part = res[:, half * cols:(half + 1) * cols]
            raw[2 * s + half] = part
            for h in range(heads):
                piece = part[:, h * HEAD_DIM:(h + 1) * HEAD_DIM]
                sq = sq + piece * piece
        @pl.when(s == 0)
        def _():
            ssq[t] = sq

        @pl.when(s > 0)
        def _():
            ssq[t] += sq

    def norm_and_send(t, g_ref):
        swap = pltpu.make_async_remote_copy(
            src_ref=ssq.at[t], dst_ref=ssq_in.at[t], send_sem=ss_s.at[t], recv_sem=ss_r.at[t],
            device_id={"sp": sibling}, device_id_type=MESH)
        swap.start()
        swap.wait_recv()
        total = jnp.sum(ssq[t] + ssq_in[t], axis=1, keepdims=True)
        scale = lax.rsqrt(total * (1.0 / width) + NORM_EPS)

        def one(idx, carry):
            g = g_ref[:, pl.ds(group_col(idx), cols)]
            table = tab[...]
            turned = pltpu.roll(table, HEAD_DIM // 2, 1)
            cos = jnp.where(first, table, turned)
            sin = jnp.where(first, -turned, table)
            parts = []
            for h in range(heads):
                at = slice(h * HEAD_DIM, (h + 1) * HEAD_DIM)
                val = raw[idx, :, at] * scale * g[:, at]
                parts.append((val * cos + pltpu.roll(val, HEAD_DIM // 2, 1) * sin).astype(BF16))
            emit(t, idx, jnp.concatenate(parts, axis=1))
            return carry

        lax.fori_loop(0, n_chip, one, 0)

    def k_step(s, carry):
        raw_step(1, s)
        w_copy(wq, s, 0).start()
        w_copy(wq, s, 1).start()
        return carry

    lax.fori_loop(0, n_step, k_step, 0)
    norm_and_send(1, kg_ref)
    for j in range(n_step, n_wo):
        wo_copy(j).start()

    def q_step(s, carry):
        raw_step(0, s)
        wo_copy(s).start()
        return carry

    lax.fori_loop(0, n_step, q_step, 0)
    norm_and_send(0, qg_ref)

    def arrivals(t):
        def one(idx, carry):
            exchange(t, idx).wait_recv()
            return carry
        lax.fori_loop(0, n_chip - 1, one, 0)

    def fill_cache(t, which, out_hbm):
        def one(b, carry):
            base = pl.multiple_of(b * rows, rows)
            block = recv[t, pl.ds(base, rows), :].astype(F32)
            for h in range(heads):
                stage[pl.ds(h, rows, stride=heads), :] = block[:, h * HEAD_DIM:(h + 1) * HEAD_DIM]
            cache[which, pl.ds(pl.multiple_of(heads * base, heads * rows), heads * rows), :] = stage[...].astype(BF16)
            return carry
        lax.fori_loop(0, n_chip, one, 0)
        last = new[t][0:1, :].astype(F32)
        rows_new = jnp.concatenate([last[:, h * HEAD_DIM:(h + 1) * HEAD_DIM] for h in range(heads)], axis=0)
        cache[which, pl.ds(heads * seq, heads), :] = rows_new.astype(BF16)
        pltpu.make_async_copy(cache.at[which], out_hbm, csem.at[which]).start()

    arrivals(2)
    fill_cache(2, 1, vc_hbm)
    arrivals(1)
    fill_cache(1, 0, kc_hbm)

    log_scale = HEAD_DIM ** -0.5 * math.log2(math.e)
    contract_last = (((1,), (1,)), ((), ()))

    for h in range(heads):
        at = slice(h * HEAD_DIM, (h + 1) * HEAD_DIM)
        qd, kd, vd = new[0][:, at], new[1][:, at], new[2][:, at]
        sc = lax.dot_general(qd, recv[1, :, at], contract_last, preferred_element_type=F32) * log_scale
        sn = jnp.sum(qd.astype(F32) * kd.astype(F32), axis=1, keepdims=True) * log_scale
        top = jnp.maximum(jnp.max(sc, axis=1, keepdims=True), sn)
        ex = jnp.exp2(sc - top)
        en = jnp.exp2(sn - top)
        inv = 1.0 / (jnp.sum(ex, axis=1, keepdims=True) + en)
        prob = (ex * inv).astype(BF16)
        prob_n = (en * inv).astype(BF16).astype(F32)
        od = jnp.dot(prob, recv[2, :, at], preferred_element_type=F32) + prob_n * vd.astype(F32)
        dsend[:, at] = od[0:1].astype(BF16).astype(F32)

    def d_copy(off, kk, to):
        return pltpu.make_async_remote_copy(
            src_ref=dsend, dst_ref=dsum.at[2 * off + core], send_sem=d_s.at[off, kk], recv_sem=d_r.at[off, core],
            device_id={"sp": to}, device_id_type=MESH)

    d_copy(0, 0, sibling).start()
    for off in range(1, n_chip):
        for kk in range(2):
            d_copy(off, kk, 2 * lax.rem(chip + off, n_chip) + kk).start()
    dsum[core] = dsend[...]

    def o_copy(i, kk, to, off_o):
        return pltpu.make_async_remote_copy(
            src_ref=osend.at[i, pl.ds(pl.multiple_of(kk * tok, tok), tok)],
            dst_ref=orecv.at[off_o, pl.ds(0, tok), pl.ds(pl.multiple_of(core * cols, cols), cols)],
            send_sem=o_s.at[i, kk], recv_sem=o_r.at[off_o, core], device_id={"sp": to}, device_id_type=MESH)

    def attend(i, carry):
        idx = lax.rem(i + n_chip - 1, n_chip)
        off_q = offset_of(idx)
        src = lax.rem(chip + n_chip - off_q, n_chip)
        off_o = lax.rem(n_chip - off_q, n_chip)

        @pl.when(i > 0)
        def _():
            exchange(0, idx).wait_recv()

        q_at = pl.ds(pl.multiple_of(src * rows, rows), rows)
        for h in range(heads):
            at = slice(h * HEAD_DIM, (h + 1) * HEAD_DIM)
            s_ref[...] = lax.dot_general(recv[0, q_at, at], recv[1, :, at], contract_last, preferred_element_type=F32)

            def soft(r, c):
                r_at = pl.ds(pl.multiple_of(r * PAD, PAD), PAD)
                sc = s_ref[r_at, :] * log_scale
                q_pos = src * rows + r * PAD + lax.broadcasted_iota(jnp.int32, sc.shape, 0)
                sc = jnp.where(q_pos >= lax.broadcasted_iota(jnp.int32, sc.shape, 1), sc, MASKED)
                ex = jnp.exp2(sc - jnp.max(sc, axis=1, keepdims=True))
                inv = 1.0 / jnp.sum(ex, axis=1, keepdims=True)
                p_ref[r_at, :] = (ex * inv).astype(BF16)
                return c

            lax.fori_loop(0, rows // PAD, soft, 0)
            osend[i, :, at] = jnp.dot(p_ref[...], recv[2, :, at], preferred_element_type=F32).astype(BF16)

        @pl.when(i > 0)
        def _():
            for kk in range(2):
                o_copy(i, kk, 2 * src + kk, off_o).start()

        @pl.when(i == 0)
        def _():
            o_copy(i, 1 - core, sibling, off_o).start()
            orecv[0, pl.ds(0, tok), pl.ds(pl.multiple_of(core * cols, cols), cols)] = osend[0, my_rows, :]
        return carry

    lax.fori_loop(0, n_chip, attend, 0)

    for j in range(n_wo):
        wo_copy(j).wait()

    zero_half = jnp.zeros((8, cols), BF16)

    def gather(i, carry):
        off_o = lax.rem(n_chip - offset_of(lax.rem(i + n_chip - 1, n_chip)), n_chip)
        src = lax.rem(chip + n_chip - off_o, n_chip)

        def wait_pair(kk):
            pltpu.make_async_remote_copy(
                src_ref=osend.at[0, pl.ds(0, tok)], dst_ref=orecv.at[off_o, pl.ds(0, tok), pl.ds(pl.multiple_of(kk * cols, cols), cols)],
                send_sem=o_s.at[0, 0], recv_sem=o_r.at[off_o, kk], device_id={"sp": sibling}, device_id_type=MESH).wait_recv()
            pltpu.make_async_remote_copy(
                src_ref=dsend, dst_ref=dsum.at[2 * off_o + kk], send_sem=d_s.at[0, 0], recv_sem=d_r.at[off_o, kk],
                device_id={"sp": sibling}, device_id_type=MESH).wait_recv()

        @pl.when(i == 0)
        def _():
            wait_pair(1 - core)

        @pl.when(i > 0)
        def _():
            wait_pair(0)
            wait_pair(1)

        d0 = jnp.broadcast_to(dsum[2 * off_o].astype(BF16), (8, cols))
        d1 = jnp.broadcast_to(dsum[2 * off_o + 1].astype(BF16), (8, cols))
        orecv[off_o, pl.ds(tok, PAD), :] = jnp.concatenate(
            [jnp.concatenate([d0, zero_half], axis=1), jnp.concatenate([zero_half, d1], axis=1)], axis=0)
        k_at = pl.ds(pl.multiple_of(src * wide, wide), wide)
        lhs = orecv[off_o]
        for j in range(n_wo):
            res = jnp.dot(lhs, pool[j, k_at, :], preferred_element_type=F32)
            parts = res[tok:tok + 8].astype(BF16).astype(F32) + res[tok + 8:].astype(BF16).astype(F32)
            n_at = slice(j * wide, (j + 1) * wide)

            @pl.when(i == 0)
            def _():
                acc[pl.ds(0, tok), n_at] = res[:tok]
                acc[pl.ds(tok, 8), n_at] = parts

            @pl.when(i > 0)
            def _():
                acc[pl.ds(0, tok), n_at] += res[:tok]
                acc[pl.ds(tok, 8), n_at] += parts
        return carry

    lax.fori_loop(0, n_chip, gather, 0)

    def finish(r, carry):
        r_at = pl.ds(pl.multiple_of(r * PAD, PAD), PAD)
        val = acc[r_at, :]
        scale = lax.rsqrt(jnp.sum(val * val, axis=1, keepdims=True) * (1.0 / width) + NORM_EPS)
        x_at = pl.ds(pl.multiple_of(core * tok + r * PAD, PAD), PAD)
        outp_ref[r_at, :] = (xs[x_at, :].astype(F32) + val * scale * pg_ref[...]).astype(BF16)
        return carry

    lax.fori_loop(0, tok // PAD, finish, 0)
    val = acc[pl.ds(tok, 8), :]
    scale = lax.rsqrt(jnp.sum(val * val, axis=1, keepdims=True) * (1.0 / width) + NORM_EPS)
    outd_ref[...] = (new_ref[...].astype(F32) + (val * scale * pg_ref[...])[0:1]).astype(BF16)

    x_send.wait_send()
    for t in range(2):
        pltpu.make_async_remote_copy(
            src_ref=ssq.at[t], dst_ref=ssq_in.at[t], send_sem=ss_s.at[t], recv_sem=ss_r.at[t],
            device_id={"sp": sibling}, device_id_type=MESH).wait_send()

    def drain(idx, carry):
        for t in range(3):
            exchange(t, idx).wait_send()
        for kk in range(2):
            o_copy(idx + 1, kk, sibling, 0).wait_send()
            d_copy(idx + 1, kk, sibling).wait_send()
        return carry

    lax.fori_loop(0, n_chip - 1, drain, 0)
    o_copy(0, 1 - core, sibling, 0).wait_send()
    d_copy(0, 0, sibling).wait_send()
    pltpu.make_async_copy(cache.at[1], vc_hbm, csem.at[1]).wait()
    pltpu.make_async_copy(cache.at[0], kc_hbm, csem.at[0]).wait()


def solution(mesh):
    n_dev = mesh.shape["sp"]

    def device_step(prompt_blk, w_q, w_k, w_v, w_o, q_norm_w, k_norm_w, post_norm_w, new_rows):
        _, tok, width = prompt_blk.shape
        n_chip = n_dev // 2
        rows, seq, cols = 2 * tok, tok * n_dev, width // n_dev
        heads = cols // HEAD_DIM
        wide = 2 * cols
        n_wo = width // wide
        table = jnp.asarray(rope_table(seq))
        vmem = pl.BlockSpec(memory_space=pltpu.VMEM)
        hbm = pl.BlockSpec(memory_space=pl.ANY)
        dma = pltpu.SemaphoreType.DMA
        cache_shape = jax.ShapeDtypeStruct((heads * (seq + 1), HEAD_DIM), BF16)
        outp, kc, vc, outd = pl.pallas_call(
            functools.partial(kernel, n_dev),
            out_shape=(jax.ShapeDtypeStruct((tok, width), BF16), cache_shape, cache_shape, jax.ShapeDtypeStruct((1, width), BF16)),
            in_specs=[hbm, vmem, hbm, hbm, hbm, hbm, vmem, vmem, vmem, hbm],
            out_specs=(vmem, hbm, hbm, vmem),
            scratch_shapes=[
                pltpu.VMEM((rows + PAD, width), BF16),
                pltpu.VMEM((n_wo, width, wide), BF16),
                pltpu.VMEM((rows + PAD, HEAD_DIM), F32),
                pltpu.VMEM((n_chip, rows + PAD, cols), F32),
                pltpu.VMEM((2, rows + PAD, HEAD_DIM), F32),
                pltpu.VMEM((2, rows + PAD, HEAD_DIM), F32),
                pltpu.VMEM((3, n_chip, rows, cols), BF16),
                pltpu.VMEM((3, seq, cols), BF16),
                pltpu.VMEM((3, PAD, cols), BF16),
                pltpu.VMEM((rows, seq), F32),
                pltpu.VMEM((rows, seq), BF16),
                pltpu.VMEM((n_chip, rows, cols), BF16),
                pltpu.VMEM((n_chip, tok + PAD, wide), BF16),
                pltpu.VMEM((1, cols), F32),
                pltpu.VMEM((n_dev, 1, cols), F32),
                pltpu.VMEM((tok + 8, width), F32),
                pltpu.VMEM((heads * rows, HEAD_DIM), F32),
                pltpu.VMEM((2, heads * (seq + 1), HEAD_DIM), BF16),
                dma(()), dma((n_chip // 2, 2)), dma((n_wo,)), dma((2,)),
                dma(()), dma(()), dma((2,)), dma((2,)),
                dma((3, n_chip)), dma((3, n_chip)),
                dma((n_chip, 2)), dma((n_chip, 2)),
                dma((n_chip, 2)), dma((n_chip, 2)),
                dma((2,)),
            ],
            compiler_params=pltpu.CompilerParams(collective_id=0, has_side_effects=True, vmem_limit_bytes=62 * 1024 * 1024),
        )(prompt_blk[0], new_rows, w_q, w_k, w_v, w_o, q_norm_w[None], k_norm_w[None], post_norm_w[None], table)
        shape = (1, seq + 1, heads, HEAD_DIM)
        return outp[None], kc.reshape(shape), vc.reshape(shape), outd

    replicated = P()
    return jax.shard_map(
        device_step, mesh=mesh,
        in_specs=(P("dp", "sp", None), replicated, replicated, replicated, replicated, replicated, replicated, replicated, P("dp", None)),
        out_specs=(P("dp", "sp", None), P("dp", None, "sp", None), P("dp", None, "sp", None), P("dp", None)),
        check_vma=False)
```

time: 212 us -> 99.8 us (0.47)
  Pallas kernels: 0 us -> 90.5 us
  matrix products: 77.5 us -> 0 us
  blocking collectives: 46.7 us -> 0 us
  waiting for transfers between devices: 37.1 us -> 0 us
  other arithmetic: 19.6 us -> 0 us
  between operations: 16.5 us -> 0.64 us
  local copies, waits for them, and re-layouts: 13.8 us -> 8.31 us
    pallas_call x0 -> x1, Pallas kernels: none -> 90.5 us  [device_step(): pl.pallas_call(functools.partial(kernel, n_dev), out_shape=(jax.ShapeDtyp...]
    dot_general x12 -> x0, matrix products: 77.5 us -> none  [the longest x2 27.6 us: project_heads(): jnp.dot(x_rows, w_mat, preferred_element_type=jnp.float32)]
    all_gather x2 -> x0, waiting for transfers between devices: 37 us -> none  [the longest x1 37 us: device_step(): v_all = lax.all_gather(v_loc, 'sp', axis=1, tiled=True)]
    psum x1 -> x0, blocking collectives: 30.7 us -> none  [device_step(): sq_total = lax.psum(sq_sums, 'sp')]
    all_gather x1 -> x0, blocking collectives: 16 us -> none  [device_step(): all_parts = lax.all_gather(part_proj, 'sp')]
    unnamed x23 -> x2, local copies, waits for them, and re-layouts: 9.53 us -> 3.21 us
    sub x1 -> x0, other arithmetic: 5.72 us -> none  [one_block(): attn_p = jax.nn.softmax(scores, axis=-1).astype(jnp.bfloat16)]
    convert_element_type x8 -> x0, other arithmetic: 4.2 us -> none  [the longest x1 1.56 us: project_heads(): apply_rope(normed.reshape(x_rows.shape[:-1] + (-1, HEAD_DIM)), cos_t, sin_t)]
  transfers between devices with their start and end apart: 2 -> 0, of which waited for: 1 -> 0; matrix products, arithmetic and copies ran while one was open for 20% -> 0% of each run, Pallas kernels for 0% -> 0%
where the time goes in v1:
time: 99.8 us; the launch traced here: 99.5 us
  Pallas kernels  90.5 us (91%)
  local copies, waits for them, and re-layouts  8.31 us (8%)
    pallas_call x1, Pallas kernels, device_step(): pl.pallas_call(functools.partial(kernel, n_dev), out_shape=(jax.ShapeDtyp...  90.5 us
    reshape x2, local copies, waits for them, and re-layouts, device_step(): return (outp[None], kc.reshape(shape), vc.reshape(shape), outd)  5.11 us
    unnamed x2, local copies, waits for them, and re-layouts  3.21 us

profile of v1, /device:TPU:21, one launch (start us, length us, event | category | flops | bytes accessed | tf_op | source)
XLA Modules:
  0.0 99.5 jit_solution(2123359540937279205)
XLA Ops:
  0.6 90.5 %shard_map.129 = (bf16[64,4096]{1,0:T(8,128)(2,1)}, bf16[2050,128]{1,0:T(8,128)(2,1)}, bf16[2050,128]{1,0:T(8,128)(2,1)}, bf16[1,4096]{1,0:T(2,128)(2,1)}) custom-call(bf16[64,4096]{1,0:T(8,128)(2,1)} %bitcast.5, bf16[1,4096]{1,0:T(2,128)(2,1)} %new_ref.1, bf16[4096,4096]{1,0:T(8,128)(2,1)} %wq.1, bf16[4096,4096]{1,0:T(8,128)(2,1)} %wk.1, ...), custom_call_target="tpu_custom_call" | custom-call | tf_op jit(solution)/shard_map/pallas_call | solution.py:388
  91.2 2.6 %reshape.14 = bf16[1,1025,2,128]{3,2,1,0:T(2,128)(2,1)} reshape(bf16[2050,128]{1,0:T(8,128)(2,1)} %get-tuple-element.9) | data formatting | bytes 1049600 | tf_op jit(solution)/shard_map/reshape | solution.py:422
  93.7 2.5 %reshape.15 = bf16[1,1025,2,128]{3,2,1,0:T(2,128)(2,1)} reshape(bf16[2050,128]{1,0:T(8,128)(2,1)} %get-tuple-element.10) | data formatting | bytes 1049600 | tf_op jit(solution)/shard_map/reshape | solution.py:422
  96.3 1.9 %copy.16 = bf16[1,64,4096]{2,1,0:T(8,128)(2,1)} copy(bf16[1,64,4096]{2,1,0:T(8,128)(2,1)} %bitcast.6) | data formatting | bytes 1048576
  98.2 1.3 %copy.17 = bf16[1,4096]{1,0:T(2,128)(2,1)} copy(bf16[1,4096]{1,0:T(2,128)(2,1)} %get-tuple-element.19) | data formatting | bytes 16384

commit v2 on v1

--- a/solution.py
+++ b/solution.py
@@ -13,6 +13,7 @@
 ROPE_THETA = 500000.0
 NORM_EPS = 1e-6
 PAD = 16
+LAG = 4
 MASKED = -1e30
 F32 = jnp.float32
 BF16 = jnp.bfloat16
@@ -27,10 +28,11 @@
     return np.concatenate([np.cos(angles), np.sin(angles)], axis=-1).astype(np.float32)
 
 
-def kernel(n_dev, x_hbm, new_ref, wq, wk, wv, wo, qg_ref, kg_ref, pg_ref, tab_hbm,
-           outp_ref, kc_hbm, vc_hbm, outd_ref,
-           xs, pool, tab, raw, ssq, ssq_in, send, recv, new, s_ref, p_ref, osend, orecv, dsend, dsum, acc, stage, cache,
-           xsem, wsem, wosem, tabsem, xs_s, xs_r, ss_s, ss_r, a_s, a_r, d_s, d_r, o_s, o_r, csem):
+def kernel(n_dev, x_hbm, new_hbm, wq, wk, wv, wo, qg_hbm, kg_hbm, pg_hbm, tab_hbm,
+           outp_hbm, kc_hbm, vc_hbm, outd_hbm,
+           new_ref, qg_ref, kg_ref, pg_ref, outp_ref, outd_ref,
+           xs, pool, tab, raw, ssq, ssq_in, send, recv, new, s_ref, p_ref, vt, osend, orecv, dsend, dsum, acc, stage, cache,
+           xsem, insem, outsem, wsem, wosem, tabsem, xs_s, xs_r, ss_s, ss_r, a_s, a_r, d_s, d_r, o_s, o_r, csem):
     tok = x_hbm.shape[0]
     width = x_hbm.shape[1]
     rows = 2 * tok
@@ -66,9 +68,10 @@
     my_rows = pl.ds(pl.multiple_of(core * tok, tok), tok)
     x_copy = pltpu.make_async_copy(x_hbm, xs.at[my_rows], xsem)
     x_copy.start()
-    for s in range(n_step):
-        w_copy(wv, s, 0).start()
-        w_copy(wv, s, 1).start()
+    smalls = [pltpu.make_async_copy(a, b, insem.at[n]) for n, (a, b) in enumerate(
+        ((new_hbm, new_ref), (qg_hbm, qg_ref), (kg_hbm, kg_ref), (pg_hbm, pg_ref)))]
+    for small in smalls:
+        small.start()
     tab_a = pltpu.make_async_copy(tab_hbm.at[pl.ds(pl.multiple_of(chip * rows, rows), rows)], tab.at[pl.ds(0, rows)], tabsem.at[0])
     tab_b = pltpu.make_async_copy(tab_hbm.at[pl.ds(seq, PAD)], tab.at[pl.ds(rows, PAD)], tabsem.at[1])
     tab_a.start()
@@ -77,14 +80,22 @@
     barrier = pltpu.get_barrier_semaphore()
     for off in range(1, n_dev):
         pl.semaphore_signal(barrier, inc=1, device_id={"sp": lax.rem(me + off, n_dev)}, device_id_type=MESH)
+    for small in smalls:
+        small.wait()
+    x_copy.wait()
+    for s in range(n_step):
+        w_copy(wv, s, 0).start()
+        w_copy(wv, s, 1).start()
     xs[pl.ds(rows, PAD), :] = jnp.broadcast_to(new_ref[...], (PAD, width))
-    x_copy.wait()
-    pl.semaphore_wait(barrier, n_dev - 1)
+    with jax.named_scope("barrier"):
+        pl.semaphore_wait(barrier, n_dev - 1)
 
     x_send = pltpu.make_async_remote_copy(
         src_ref=xs.at[my_rows], dst_ref=xs.at[my_rows], send_sem=xs_s, recv_sem=xs_r, device_id={"sp": sibling}, device_id_type=MESH)
     x_send.start()
-    x_send.wait_recv()
+    acc[...] = jnp.zeros_like(acc)
+    with jax.named_scope('x_arrive'):
+        x_send.wait_recv()
 
     own_rows = pl.ds(pl.multiple_of(chip * rows, rows), rows)
 
@@ -118,7 +129,8 @@
             emit(2, 2 * s + half, res[:, half * cols:(half + 1) * cols].astype(BF16))
         return carry
 
-    lax.fori_loop(0, n_step, v_step, 0)
+    with jax.named_scope('v_proj'):
+        lax.fori_loop(0, n_step, v_step, 0)
     tab_a.wait()
     tab_b.wait()
 
@@ -173,8 +185,10 @@
         w_copy(wq, s, 1).start()
         return carry
 
-    lax.fori_loop(0, n_step, k_step, 0)
-    norm_and_send(1, kg_ref)
+    with jax.named_scope('k_proj'):
+        lax.fori_loop(0, n_step, k_step, 0)
+    with jax.named_scope('k_norm'):
+        norm_and_send(1, kg_ref)
     for j in range(n_step, n_wo):
         wo_copy(j).start()
 
@@ -183,8 +197,10 @@
         wo_copy(s).start()
         return carry
 
-    lax.fori_loop(0, n_step, q_step, 0)
-    norm_and_send(0, qg_ref)
+    with jax.named_scope('q_proj'):
+        lax.fori_loop(0, n_step, q_step, 0)
+    with jax.named_scope('q_norm'):
+        norm_and_send(0, qg_ref)
 
     def arrivals(t):
         def one(idx, carry):
@@ -206,10 +222,17 @@
         cache[which, pl.ds(heads * seq, heads), :] = rows_new.astype(BF16)
         pltpu.make_async_copy(cache.at[which], out_hbm, csem.at[which]).start()
 
-    arrivals(2)
-    fill_cache(2, 1, vc_hbm)
-    arrivals(1)
-    fill_cache(1, 0, kc_hbm)
+    with jax.named_scope("v_arrive"):
+        arrivals(2)
+    with jax.named_scope("v_cache"):
+        fill_cache(2, 1, vc_hbm)
+        for b in range(n_chip):
+            for h in range(heads):
+                vt[h, :, b * rows:(b + 1) * rows] = recv[2, b * rows:(b + 1) * rows, h * HEAD_DIM:(h + 1) * HEAD_DIM].astype(F32).T.astype(BF16)
+    with jax.named_scope("k_arrive"):
+        arrivals(1)
+    with jax.named_scope("k_cache"):
+        fill_cache(1, 0, kc_hbm)
 
     log_scale = HEAD_DIM ** -0.5 * math.log2(math.e)
     contract_last = (((1,), (1,)), ((), ()))
@@ -245,7 +268,10 @@
             dst_ref=orecv.at[off_o, pl.ds(0, tok), pl.ds(pl.multiple_of(core * cols, cols), cols)],
             send_sem=o_s.at[i, kk], recv_sem=o_r.at[off_o, core], device_id={"sp": to}, device_id_type=MESH)
 
-    def attend(i, carry):
+    def fold(block, op):
+        return op(block.reshape(block.shape[0] // 8, 8, block.shape[1]), axis=0)
+
+    def attend(i):
         idx = lax.rem(i + n_chip - 1, n_chip)
         off_q = offset_of(idx)
         src = lax.rem(chip + n_chip - off_q, n_chip)
@@ -253,25 +279,35 @@
 
         @pl.when(i > 0)
         def _():
-            exchange(0, idx).wait_recv()
-
-        q_at = pl.ds(pl.multiple_of(src * rows, rows), rows)
+            with jax.named_scope("q_arrive"):
+                exchange(0, idx).wait_recv()
+
+        src_at = pl.ds(pl.multiple_of(src * rows, rows), rows)
+        causal = lax.broadcasted_iota(jnp.int32, (rows, rows), 0) <= lax.broadcasted_iota(jnp.int32, (rows, rows), 1)
+        blocks = [slice(kb * rows, (kb + 1) * rows) for kb in range(n_chip)]
+        tops = []
         for h in range(heads):
             at = slice(h * HEAD_DIM, (h + 1) * HEAD_DIM)
-            s_ref[...] = lax.dot_general(recv[0, q_at, at], recv[1, :, at], contract_last, preferred_element_type=F32)
-
-            def soft(r, c):
-                r_at = pl.ds(pl.multiple_of(r * PAD, PAD), PAD)
-                sc = s_ref[r_at, :] * log_scale
-                q_pos = src * rows + r * PAD + lax.broadcasted_iota(jnp.int32, sc.shape, 0)
-                sc = jnp.where(q_pos >= lax.broadcasted_iota(jnp.int32, sc.shape, 1), sc, MASKED)
-                ex = jnp.exp2(sc - jnp.max(sc, axis=1, keepdims=True))
-                inv = 1.0 / jnp.sum(ex, axis=1, keepdims=True)
-                p_ref[r_at, :] = (ex * inv).astype(BF16)
-                return c
-
-            lax.fori_loop(0, rows // PAD, soft, 0)
-            osend[i, :, at] = jnp.dot(p_ref[...], recv[2, :, at], preferred_element_type=F32).astype(BF16)
+            sc = lax.dot_general(recv[1, :, at], recv[0, src_at, at], contract_last, preferred_element_type=F32)
+            s_ref[h] = sc
+            top = jnp.full((8, rows), -jnp.inf, F32)
+            for kb in range(n_chip):
+                top = jnp.maximum(top, fold(sc[blocks[kb]], jnp.max) + jnp.where(kb < src, 0.0, -jnp.inf))
+            tops.append(top)
+        for h in range(heads):
+            at = slice(h * HEAD_DIM, (h + 1) * HEAD_DIM)
+            own = jnp.where(causal, s_ref[h, src_at, :], -jnp.inf)
+            s_ref[h, src_at, :] = own
+            top = jnp.max(jnp.maximum(tops[h], fold(own, jnp.max)), axis=0, keepdims=True) * log_scale
+            total = jnp.zeros((8, rows), F32)
+            for kb in range(n_chip):
+                ex = jnp.exp2(s_ref[h, blocks[kb], :] * log_scale + (jnp.where(kb <= src, 0.0, -jnp.inf) - top))
+                s_ref[h, blocks[kb], :] = ex
+                total = total + fold(ex, jnp.sum)
+            inv = 1.0 / jnp.sum(total, axis=0, keepdims=True)
+            for kb in range(n_chip):
+                p_ref[h, blocks[kb], :] = (s_ref[h, blocks[kb], :] * inv).astype(BF16)
+            osend[i, :, at] = jnp.dot(vt[h], p_ref[h], preferred_element_type=F32).T.astype(BF16)
 
         @pl.when(i > 0)
         def _():
@@ -282,16 +318,10 @@
         def _():
             o_copy(i, 1 - core, sibling, off_o).start()
             orecv[0, pl.ds(0, tok), pl.ds(pl.multiple_of(core * cols, cols), cols)] = osend[0, my_rows, :]
-        return carry
-
-    lax.fori_loop(0, n_chip, attend, 0)
-
-    for j in range(n_wo):
-        wo_copy(j).wait()
 
     zero_half = jnp.zeros((8, cols), BF16)
 
-    def gather(i, carry):
+    def gather(i):
         off_o = lax.rem(n_chip - offset_of(lax.rem(i + n_chip - 1, n_chip)), n_chip)
         src = lax.rem(chip + n_chip - off_o, n_chip)
 
@@ -309,8 +339,9 @@
 
         @pl.when(i > 0)
         def _():
-            wait_pair(0)
-            wait_pair(1)
+            with jax.named_scope("o_arrive"):
+                wait_pair(0)
+                wait_pair(1)
 
         d0 = jnp.broadcast_to(dsum[2 * off_o].astype(BF16), (8, cols))
         d1 = jnp.broadcast_to(dsum[2 * off_o + 1].astype(BF16), (8, cols))
@@ -322,19 +353,31 @@
             res = jnp.dot(lhs, pool[j, k_at, :], preferred_element_type=F32)
             parts = res[tok:tok + 8].astype(BF16).astype(F32) + res[tok + 8:].astype(BF16).astype(F32)
             n_at = slice(j * wide, (j + 1) * wide)
-
-            @pl.when(i == 0)
-            def _():
-                acc[pl.ds(0, tok), n_at] = res[:tok]
-                acc[pl.ds(tok, 8), n_at] = parts
-
-            @pl.when(i > 0)
-            def _():
-                acc[pl.ds(0, tok), n_at] += res[:tok]
-                acc[pl.ds(tok, 8), n_at] += parts
+            acc[pl.ds(0, tok), n_at] += res[:tok]
+            acc[pl.ds(tok, 8), n_at] += parts
+
+    def both(i, carry):
+        @pl.when(i < n_chip)
+        def _():
+            with jax.named_scope("attend"):
+                attend(i)
+
+        @pl.when(i == LAG)
+        def _():
+            for j in range(n_wo):
+                wo_copy(j).wait()
+
+        @pl.when(i >= LAG)
+        def _():
+            with jax.named_scope("gather"):
+                gather(i - LAG)
         return carry
 
-    lax.fori_loop(0, n_chip, gather, 0)
+    lax.fori_loop(0, n_chip + LAG, both, 0)
+
+    def outp_copy(r):
+        r_at = pl.ds(pl.multiple_of(r * PAD, PAD), PAD)
+        return pltpu.make_async_copy(outp_ref.at[r_at], outp_hbm.at[r_at], outsem.at[r])
 
     def finish(r, carry):
         r_at = pl.ds(pl.multiple_of(r * PAD, PAD), PAD)
@@ -342,12 +385,16 @@
         scale = lax.rsqrt(jnp.sum(val * val, axis=1, keepdims=True) * (1.0 / width) + NORM_EPS)
         x_at = pl.ds(pl.multiple_of(core * tok + r * PAD, PAD), PAD)
         outp_ref[r_at, :] = (xs[x_at, :].astype(F32) + val * scale * pg_ref[...]).astype(BF16)
+        outp_copy(r).start()
         return carry
 
-    lax.fori_loop(0, tok // PAD, finish, 0)
-    val = acc[pl.ds(tok, 8), :]
-    scale = lax.rsqrt(jnp.sum(val * val, axis=1, keepdims=True) * (1.0 / width) + NORM_EPS)
-    outd_ref[...] = (new_ref[...].astype(F32) + (val * scale * pg_ref[...])[0:1]).astype(BF16)
+    with jax.named_scope("finish"):
+        lax.fori_loop(0, tok // PAD, finish, 0)
+        val = acc[pl.ds(tok, 8), :]
+        scale = lax.rsqrt(jnp.sum(val * val, axis=1, keepdims=True) * (1.0 / width) + NORM_EPS)
+        outd_ref[...] = (new_ref[...].astype(F32) + (val * scale * pg_ref[...])[0:1]).astype(BF16)
+        outd_copy = pltpu.make_async_copy(outd_ref, outd_hbm, insem.at[0])
+        outd_copy.start()
 
     x_send.wait_send()
     for t in range(2):
@@ -368,6 +415,23 @@
     d_copy(0, 0, sibling).wait_send()
     pltpu.make_async_copy(cache.at[1], vc_hbm, csem.at[1]).wait()
     pltpu.make_async_copy(cache.at[0], kc_hbm, csem.at[0]).wait()
+    for r in range(tok // PAD):
+        outp_copy(r).wait()
+    outd_copy.wait()
+
+
+def hand_over(outp_in, kc_in, vc_in, outd_in, outp, kc, vc, outd, b0, b1, b2, b3, sem):
+    ins = [pltpu.make_async_copy(a, b, sem.at[0, n]) for n, (a, b) in enumerate(
+        ((outp_in, b0), (kc_in, b1), (vc_in, b2), (outd_in, b3)))]
+    outs = [pltpu.make_async_copy(a, b, sem.at[1, n]) for n, (a, b) in enumerate(
+        ((b0, outp), (b1, kc.reshape(b1.shape)), (b2, vc.reshape(b2.shape)), (b3, outd)))]
+    for one in ins:
+        one.start()
+    for a, b in zip(ins, outs):
+        a.wait()
+        b.start()
+    for one in outs:
+        one.wait()
 
 
 def solution(mesh):
@@ -381,16 +445,21 @@
         wide = 2 * cols
         n_wo = width // wide
         table = jnp.asarray(rope_table(seq))
-        vmem = pl.BlockSpec(memory_space=pltpu.VMEM)
         hbm = pl.BlockSpec(memory_space=pl.ANY)
         dma = pltpu.SemaphoreType.DMA
         cache_shape = jax.ShapeDtypeStruct((heads * (seq + 1), HEAD_DIM), BF16)
         outp, kc, vc, outd = pl.pallas_call(
             functools.partial(kernel, n_dev),
             out_shape=(jax.ShapeDtypeStruct((tok, width), BF16), cache_shape, cache_shape, jax.ShapeDtypeStruct((1, width), BF16)),
-            in_specs=[hbm, vmem, hbm, hbm, hbm, hbm, vmem, vmem, vmem, hbm],
-            out_specs=(vmem, hbm, hbm, vmem),
+            in_specs=[hbm] * 10,
+            out_specs=(hbm,) * 4,
             scratch_shapes=[
+                pltpu.VMEM((1, width), BF16),
+                pltpu.VMEM((1, width), F32),
+                pltpu.VMEM((1, width), F32),
+                pltpu.VMEM((1, width), F32),
+                pltpu.VMEM((tok, width), BF16),
+                pltpu.VMEM((1, width), BF16),
                 pltpu.VMEM((rows + PAD, width), BF16),
                 pltpu.VMEM((n_wo, width, wide), BF16),
                 pltpu.VMEM((rows + PAD, HEAD_DIM), F32),
@@ -400,8 +469,9 @@
                 pltpu.VMEM((3, n_chip, rows, cols), BF16),
                 pltpu.VMEM((3, seq, cols), BF16),
                 pltpu.VMEM((3, PAD, cols), BF16),
-                pltpu.VMEM((rows, seq), F32),
-                pltpu.VMEM((rows, seq), BF16),
+                pltpu.VMEM((heads, seq, rows), F32),
+                pltpu.VMEM((heads, seq, rows), BF16),
+                pltpu.VMEM((heads, HEAD_DIM, seq), BF16),
                 pltpu.VMEM((n_chip, rows, cols), BF16),
                 pltpu.VMEM((n_chip, tok + PAD, wide), BF16),
                 pltpu.VMEM((1, cols), F32),
@@ -409,7 +479,7 @@
                 pltpu.VMEM((tok + 8, width), F32),
                 pltpu.VMEM((heads * rows, HEAD_DIM), F32),
                 pltpu.VMEM((2, heads * (seq + 1), HEAD_DIM), BF16),
-                dma(()), dma((n_chip // 2, 2)), dma((n_wo,)), dma((2,)),
+                dma(()), dma((4,)), dma((tok // PAD,)), dma((n_chip // 2, 2)), dma((n_wo,)), dma((2,)),
                 dma(()), dma(()), dma((2,)), dma((2,)),
                 dma((3, n_chip)), dma((3, n_chip)),
                 dma((n_chip, 2)), dma((n_chip, 2)),
@@ -418,8 +488,16 @@
             ],
             compiler_params=pltpu.CompilerParams(collective_id=0, has_side_effects=True, vmem_limit_bytes=62 * 1024 * 1024),
         )(prompt_blk[0], new_rows, w_q, w_k, w_v, w_o, q_norm_w[None], k_norm_w[None], post_norm_w[None], table)
-        shape = (1, seq + 1, heads, HEAD_DIM)
-        return outp[None], kc.reshape(shape), vc.reshape(shape), outd
+        shape = (seq + 1, heads, HEAD_DIM)
+        outs = pl.pallas_call(
+            hand_over,
+            out_shape=(jax.ShapeDtypeStruct((tok, width), BF16), jax.ShapeDtypeStruct(shape, BF16),
+                       jax.ShapeDtypeStruct(shape, BF16), jax.ShapeDtypeStruct((1, width), BF16)),
+            in_specs=[hbm] * 4,
+            out_specs=(hbm,) * 4,
+            scratch_shapes=[pltpu.VMEM(a.shape, BF16) for a in (outp, kc, vc, outd)] + [dma((2, 4))],
+        )(outp, kc, vc, outd)
+        return outs[0][None], outs[1][None], outs[2][None], outs[3]
 
     replicated = P()
     return jax.shard_map(

time: 99.8 us -> 69.7 us (0.70)
  Pallas kernels: 90.5 us -> 68.9 us
  local copies, waits for them, and re-layouts: 8.31 us -> 0 us
    pallas_call x1, Pallas kernels: 90.5 us -> 66.6 us  [device_step(): pl.pallas_call(functools.partial(kernel, n_dev), out_shape=(jax.ShapeDtyp...]
    reshape x2 -> x0, local copies, waits for them, and re-layouts: 5.11 us -> none  [device_step(): return (outp[None], kc.reshape(shape), vc.reshape(shape), outd)]
    unnamed x2 -> x0, local copies, waits for them, and re-layouts: 3.21 us -> none
    pallas_call x0 -> x1, Pallas kernels: none -> 2.25 us  [device_step(): pl.pallas_call(hand_over, out_shape=(jax.ShapeDtypeStruct((tok, width), B...]
where the time goes in v2:
time: 69.7 us; the launch traced here: 69.5 us
  Pallas kernels  68.9 us (99%)
    pallas_call x1, Pallas kernels, device_step(): pl.pallas_call(functools.partial(kernel, n_dev), out_shape=(jax.ShapeDtyp...  66.6 us
    pallas_call x1, Pallas kernels, device_step(): pl.pallas_call(hand_over, out_shape=(jax.ShapeDtypeStruct((tok, width), B...  2.25 us

profile of v2, /device:TPU:21, one launch (start us, length us, event | category | flops | bytes accessed | tf_op | source)
XLA Modules:
  0.0 69.5 jit_solution(13817441356252999692)
XLA Ops:
  0.6 66.6 %shard_map.129 = (bf16[64,4096]{1,0:T(8,128)(2,1)}, bf16[2050,128]{1,0:T(8,128)(2,1)}, bf16[2050,128]{1,0:T(8,128)(2,1)}, bf16[1,4096]{1,0:T(2,128)(2,1)}) custom-call(bf16[64,4096]{1,0:T(8,128)(2,1)} %bitcast.7, bf16[1,4096]{1,0:T(2,128)(2,1)} %new_hbm.1, bf16[4096,4096]{1,0:T(8,128)(2,1)} %wq.1, bf16[4096,4096]{1,0:T(8,128)(2,1)} %wk.1, ...), custom_call_target="tpu_custom_call" | custom-call | tf_op jit(solution)/shard_map/pallas_call | solution.py:451
  67.3 2.3 %shard_map.130 = (bf16[64,4096]{1,0:T(8,128)(2,1)}, bf16[1025,2,128]{2,1,0:T(2,128)(2,1)}, bf16[1025,2,128]{2,1,0:T(2,128)(2,1)}, bf16[1,4096]{1,0:T(2,128)(2,1)}) custom-call(bf16[64,4096]{1,0:T(8,128)(2,1)} %get-tuple-element.12.outp_in, bf16[2050,128]{1,0:T(8,128)(2,1)} %get-tuple-element.13.kc_in, bf16[2050,128]{1,0:T(8,128)(2,1)} %get-tuple-element.14.vc_in, ...), custom_call_target="tpu_custom_call" | custom-call | tf_op jit(solution)/shard_map/pallas_call | solution.py:492

commit v3 on v2

--- a/solution.py
+++ b/solution.py
@@ -13,7 +13,8 @@
 ROPE_THETA = 500000.0
 NORM_EPS = 1e-6
 PAD = 16
-LAG = 4
+VMEM_MIB = 50
+LAG = 6
 MASKED = -1e30
 F32 = jnp.float32
 BF16 = jnp.bfloat16
@@ -29,10 +30,10 @@
 
 
 def kernel(n_dev, x_hbm, new_hbm, wq, wk, wv, wo, qg_hbm, kg_hbm, pg_hbm, tab_hbm,
-           outp_hbm, kc_hbm, vc_hbm, outd_hbm,
-           new_ref, qg_ref, kg_ref, pg_ref, outp_ref, outd_ref,
-           xs, pool, tab, raw, ssq, ssq_in, send, recv, new, s_ref, p_ref, vt, osend, orecv, dsend, dsum, acc, stage, cache,
-           xsem, insem, outsem, wsem, wosem, tabsem, xs_s, xs_r, ss_s, ss_r, a_s, a_r, d_s, d_r, o_s, o_r, csem):
+           outp_ref, kc_ref, vc_ref, outd_ref,
+           new_ref, qg_ref, kg_ref, pg_ref,
+           xs, pool, tab, raw, ssq, ssq_in, send, recv, new, s_ref, p_ref, vt, osend, orecv, dsend, dsum, acc, stage,
+           xsem, insem, wsem, wosem, tabsem, xs_s, xs_r, ss_s, ss_r, a_s, a_r, d_s, d_r, o_s, o_r):
     tok = x_hbm.shape[0]
     width = x_hbm.shape[1]
     rows = 2 * tok
@@ -70,6 +71,8 @@
     x_copy.start()
     smalls = [pltpu.make_async_copy(a, b, insem.at[n]) for n, (a, b) in enumerate(
         ((new_hbm, new_ref), (qg_hbm, qg_ref), (kg_hbm, kg_ref), (pg_hbm, pg_ref)))]
+    w_copy(wv, 0, 0).start()
+    w_copy(wv, 0, 1).start()
     for small in smalls:
         small.start()
     tab_a = pltpu.make_async_copy(tab_hbm.at[pl.ds(pl.multiple_of(chip * rows, rows), rows)], tab.at[pl.ds(0, rows)], tabsem.at[0])
@@ -80,22 +83,10 @@
     barrier = pltpu.get_barrier_semaphore()
     for off in range(1, n_dev):
         pl.semaphore_signal(barrier, inc=1, device_id={"sp": lax.rem(me + off, n_dev)}, device_id_type=MESH)
-    for small in smalls:
-        small.wait()
     x_copy.wait()
-    for s in range(n_step):
+    for s in range(1, n_step):
         w_copy(wv, s, 0).start()
         w_copy(wv, s, 1).start()
-    xs[pl.ds(rows, PAD), :] = jnp.broadcast_to(new_ref[...], (PAD, width))
-    with jax.named_scope("barrier"):
-        pl.semaphore_wait(barrier, n_dev - 1)
-
-    x_send = pltpu.make_async_remote_copy(
-        src_ref=xs.at[my_rows], dst_ref=xs.at[my_rows], send_sem=xs_s, recv_sem=xs_r, device_id={"sp": sibling}, device_id_type=MESH)
-    x_send.start()
-    acc[...] = jnp.zeros_like(acc)
-    with jax.named_scope('x_arrive'):
-        x_send.wait_recv()
 
     own_rows = pl.ds(pl.multiple_of(chip * rows, rows), rows)
 
@@ -120,6 +111,37 @@
         w_copy(wv, s, 0).wait()
         w_copy(wv, s, 1).wait()
         return jnp.dot(xs[...], pool[s], preferred_element_type=F32)
+
+    def half_exchange(idx, which, row):
+        dest = lax.rem(chip + offset_of(idx), n_chip)
+        at = pl.ds(pl.multiple_of(which * tok, tok), tok)
+        return pltpu.make_async_remote_copy(
+            src_ref=send.at[2, idx, at], dst_ref=recv.at[2, pl.ds(pl.multiple_of(chip * rows + which * tok, tok), tok)],
+            send_sem=a_s.at[row, idx], recv_sem=a_r.at[row, idx], device_id={"sp": 2 * dest + core}, device_id_type=MESH)
+
+    def half_project(which):
+        at = pl.ds(pl.multiple_of(which * tok, tok), tok)
+        res = jnp.dot(xs[at, :], pool[0], preferred_element_type=F32).astype(BF16)
+        for idx in range(2):
+            send[2, idx, at, :] = res[:, idx * cols:(idx + 1) * cols]
+
+    w_copy(wv, 0, 0).wait()
+    w_copy(wv, 0, 1).wait()
+    with jax.named_scope("v_first"):
+        half_project(core)
+    with jax.named_scope("barrier"):
+        pl.semaphore_wait(barrier, n_dev - 1)
+    x_send = pltpu.make_async_remote_copy(
+        src_ref=xs.at[my_rows], dst_ref=xs.at[my_rows], send_sem=xs_s, recv_sem=xs_r, device_id={"sp": sibling}, device_id_type=MESH)
+    x_send.start()
+    for idx in range(2):
+        half_exchange(idx, core, 3).start()
+    for small in smalls:
+        small.wait()
+    xs[pl.ds(rows, PAD), :] = jnp.broadcast_to(new_ref[...], (PAD, width))
+    acc[...] = jnp.zeros_like(acc)
+    with jax.named_scope("x_arrive"):
+        x_send.wait_recv()
 
     def v_step(s, carry):
         res = project(s)
@@ -130,14 +152,20 @@
         return carry
 
     with jax.named_scope('v_proj'):
-        lax.fori_loop(0, n_step, v_step, 0)
+        lax.fori_loop(1, n_step, v_step, 0)
+        half_project(1 - core)
+        for idx in range(2):
+            half_exchange(idx, 1 - core, 2).start()
+        w_copy(wk, 0, 0).start()
+        w_copy(wk, 0, 1).start()
     tab_a.wait()
     tab_b.wait()
 
     lane = lax.broadcasted_iota(jnp.int32, (rows + PAD, HEAD_DIM), 1)
     first = lane < HEAD_DIM // 2
 
-    def raw_step(t, s):
+    def raw_step(t, i):
+        s = lax.rem(i + 1, n_step)
         res = project(s)
         sq = jnp.zeros((rows + PAD, HEAD_DIM), F32)
         for half in range(2):
@@ -146,13 +174,15 @@
             for h in range(heads):
                 piece = part[:, h * HEAD_DIM:(h + 1) * HEAD_DIM]
                 sq = sq + piece * piece
-        @pl.when(s == 0)
+        @pl.when(i == 0)
         def _():
             ssq[t] = sq
 
-        @pl.when(s > 0)
+        @pl.when(i > 0)
         def _():
             ssq[t] += sq
+
+        return s
 
     def norm_and_send(t, g_ref):
         swap = pltpu.make_async_remote_copy(
@@ -179,8 +209,8 @@
 
         lax.fori_loop(0, n_chip, one, 0)
 
-    def k_step(s, carry):
-        raw_step(1, s)
+    def k_step(i, carry):
+        s = raw_step(1, i)
         w_copy(wq, s, 0).start()
         w_copy(wq, s, 1).start()
         return carry
@@ -192,8 +222,8 @@
     for j in range(n_step, n_wo):
         wo_copy(j).start()
 
-    def q_step(s, carry):
-        raw_step(0, s)
+    def q_step(i, carry):
+        s = raw_step(0, i)
         wo_copy(s).start()
         return carry
 
@@ -202,37 +232,39 @@
     with jax.named_scope('q_norm'):
         norm_and_send(0, qg_ref)
 
-    def arrivals(t):
+    def arrivals(t, start=0):
         def one(idx, carry):
             exchange(t, idx).wait_recv()
             return carry
-        lax.fori_loop(0, n_chip - 1, one, 0)
-
-    def fill_cache(t, which, out_hbm):
+        lax.fori_loop(start, n_chip - 1, one, 0)
+
+    def fill_cache(t, cache):
         def one(b, carry):
             base = pl.multiple_of(b * rows, rows)
             block = recv[t, pl.ds(base, rows), :].astype(F32)
             for h in range(heads):
                 stage[pl.ds(h, rows, stride=heads), :] = block[:, h * HEAD_DIM:(h + 1) * HEAD_DIM]
-            cache[which, pl.ds(pl.multiple_of(heads * base, heads * rows), heads * rows), :] = stage[...].astype(BF16)
+            cache[pl.ds(pl.multiple_of(heads * base, heads * rows), heads * rows), :] = stage[...].astype(BF16)
             return carry
         lax.fori_loop(0, n_chip, one, 0)
         last = new[t][0:1, :].astype(F32)
         rows_new = jnp.concatenate([last[:, h * HEAD_DIM:(h + 1) * HEAD_DIM] for h in range(heads)], axis=0)
-        cache[which, pl.ds(heads * seq, heads), :] = rows_new.astype(BF16)
-        pltpu.make_async_copy(cache.at[which], out_hbm, csem.at[which]).start()
+        cache[pl.ds(heads * seq, heads), :] = rows_new.astype(BF16)
 
     with jax.named_scope("v_arrive"):
-        arrivals(2)
+        for idx in range(2):
+            half_exchange(idx, core, 3).wait_recv()
+            half_exchange(idx, 1 - core, 2).wait_recv()
+        arrivals(2, 2)
     with jax.named_scope("v_cache"):
-        fill_cache(2, 1, vc_hbm)
+        fill_cache(2, vc_ref)
         for b in range(n_chip):
             for h in range(heads):
                 vt[h, :, b * rows:(b + 1) * rows] = recv[2, b * rows:(b + 1) * rows, h * HEAD_DIM:(h + 1) * HEAD_DIM].astype(F32).T.astype(BF16)
     with jax.named_scope("k_arrive"):
         arrivals(1)
     with jax.named_scope("k_cache"):
-        fill_cache(1, 0, kc_hbm)
+        fill_cache(1, kc_ref)
 
     log_scale = HEAD_DIM ** -0.5 * math.log2(math.e)
     contract_last = (((1,), (1,)), ((), ()))
@@ -356,6 +388,31 @@
             acc[pl.ds(0, tok), n_at] += res[:tok]
             acc[pl.ds(tok, 8), n_at] += parts
 
+    def drain_early():
+        x_send.wait_send()
+        for t in range(2):
+            pltpu.make_async_remote_copy(
+                src_ref=ssq.at[t], dst_ref=ssq_in.at[t], send_sem=ss_s.at[t], recv_sem=ss_r.at[t],
+                device_id={"sp": sibling}, device_id_type=MESH).wait_send()
+
+        def drain(idx, carry):
+            for t in range(2):
+                exchange(t, idx).wait_send()
+
+            @pl.when(idx >= 2)
+            def _():
+                exchange(2, idx).wait_send()
+
+            for kk in range(2):
+                d_copy(idx + 1, kk, sibling).wait_send()
+            return carry
+
+        lax.fori_loop(0, n_chip - 1, drain, 0)
+        for idx in range(2):
+            half_exchange(idx, core, 3).wait_send()
+            half_exchange(idx, 1 - core, 2).wait_send()
+        d_copy(0, 0, sibling).wait_send()
+
     def both(i, carry):
         @pl.when(i < n_chip)
         def _():
@@ -366,6 +423,7 @@
         def _():
             for j in range(n_wo):
                 wo_copy(j).wait()
+            drain_early()
 
         @pl.when(i >= LAG)
         def _():
@@ -374,10 +432,6 @@
         return carry
 
     lax.fori_loop(0, n_chip + LAG, both, 0)
-
-    def outp_copy(r):
-        r_at = pl.ds(pl.multiple_of(r * PAD, PAD), PAD)
-        return pltpu.make_async_copy(outp_ref.at[r_at], outp_hbm.at[r_at], outsem.at[r])
 
     def finish(r, carry):
         r_at = pl.ds(pl.multiple_of(r * PAD, PAD), PAD)
@@ -385,7 +439,6 @@
         scale = lax.rsqrt(jnp.sum(val * val, axis=1, keepdims=True) * (1.0 / width) + NORM_EPS)
         x_at = pl.ds(pl.multiple_of(core * tok + r * PAD, PAD), PAD)
         outp_ref[r_at, :] = (xs[x_at, :].astype(F32) + val * scale * pg_ref[...]).astype(BF16)
-        outp_copy(r).start()
         return carry
 
     with jax.named_scope("finish"):
@@ -393,43 +446,21 @@
         val = acc[pl.ds(tok, 8), :]
         scale = lax.rsqrt(jnp.sum(val * val, axis=1, keepdims=True) * (1.0 / width) + NORM_EPS)
         outd_ref[...] = (new_ref[...].astype(F32) + (val * scale * pg_ref[...])[0:1]).astype(BF16)
-        outd_copy = pltpu.make_async_copy(outd_ref, outd_hbm, insem.at[0])
-        outd_copy.start()
-
-    x_send.wait_send()
-    for t in range(2):
-        pltpu.make_async_remote_copy(
-            src_ref=ssq.at[t], dst_ref=ssq_in.at[t], send_sem=ss_s.at[t], recv_sem=ss_r.at[t],
-            device_id={"sp": sibling}, device_id_type=MESH).wait_send()
-
-    def drain(idx, carry):
-        for t in range(3):
-            exchange(t, idx).wait_send()
+
+    def drain_o(idx, carry):
         for kk in range(2):
             o_copy(idx + 1, kk, sibling, 0).wait_send()
-            d_copy(idx + 1, kk, sibling).wait_send()
         return carry
 
-    lax.fori_loop(0, n_chip - 1, drain, 0)
+    lax.fori_loop(0, n_chip - 1, drain_o, 0)
     o_copy(0, 1 - core, sibling, 0).wait_send()
-    d_copy(0, 0, sibling).wait_send()
-    pltpu.make_async_copy(cache.at[1], vc_hbm, csem.at[1]).wait()
-    pltpu.make_async_copy(cache.at[0], kc_hbm, csem.at[0]).wait()
-    for r in range(tok // PAD):
-        outp_copy(r).wait()
-    outd_copy.wait()
-
-
-def hand_over(outp_in, kc_in, vc_in, outd_in, outp, kc, vc, outd, b0, b1, b2, b3, sem):
-    ins = [pltpu.make_async_copy(a, b, sem.at[0, n]) for n, (a, b) in enumerate(
-        ((outp_in, b0), (kc_in, b1), (vc_in, b2), (outd_in, b3)))]
-    outs = [pltpu.make_async_copy(a, b, sem.at[1, n]) for n, (a, b) in enumerate(
-        ((b0, outp), (b1, kc.reshape(b1.shape)), (b2, vc.reshape(b2.shape)), (b3, outd)))]
-    for one in ins:
+
+
+def hand_over(outp_in, kc_in, vc_in, outd_in, outp, kc, vc, outd, sem):
+    outs = [pltpu.make_async_copy(a, b, sem.at[n]) for n, (a, b) in enumerate(
+        ((outp_in, outp), (kc_in, kc.reshape(kc_in.shape)), (vc_in, vc.reshape(vc_in.shape)), (outd_in, outd)))]
+    for one in outs:
         one.start()
-    for a, b in zip(ins, outs):
-        a.wait()
-        b.start()
     for one in outs:
         one.wait()
 
@@ -445,21 +476,24 @@
         wide = 2 * cols
         n_wo = width // wide
         table = jnp.asarray(rope_table(seq))
-        hbm = pl.BlockSpec(memory_space=pl.ANY)
+        hbm = pl.BlockSpec(memory_space=pltpu.HBM)
+        vmem = pl.BlockSpec(memory_space=pltpu.VMEM)
         dma = pltpu.SemaphoreType.DMA
         cache_shape = jax.ShapeDtypeStruct((heads * (seq + 1), HEAD_DIM), BF16)
+
+        def keep(value):
+            return pltpu.with_memory_space_constraint(value, pltpu.HBM)
+
         outp, kc, vc, outd = pl.pallas_call(
             functools.partial(kernel, n_dev),
             out_shape=(jax.ShapeDtypeStruct((tok, width), BF16), cache_shape, cache_shape, jax.ShapeDtypeStruct((1, width), BF16)),
             in_specs=[hbm] * 10,
-            out_specs=(hbm,) * 4,
+            out_specs=(vmem,) * 4,
             scratch_shapes=[
                 pltpu.VMEM((1, width), BF16),
                 pltpu.VMEM((1, width), F32),
                 pltpu.VMEM((1, width), F32),
                 pltpu.VMEM((1, width), F32),
-                pltpu.VMEM((tok, width), BF16),
-                pltpu.VMEM((1, width), BF16),
                 pltpu.VMEM((rows + PAD, width), BF16),
                 pltpu.VMEM((n_wo, width, wide), BF16),
                 pltpu.VMEM((rows + PAD, HEAD_DIM), F32),
@@ -478,24 +512,23 @@
                 pltpu.VMEM((n_dev, 1, cols), F32),
                 pltpu.VMEM((tok + 8, width), F32),
                 pltpu.VMEM((heads * rows, HEAD_DIM), F32),
-                pltpu.VMEM((2, heads * (seq + 1), HEAD_DIM), BF16),
-                dma(()), dma((4,)), dma((tok // PAD,)), dma((n_chip // 2, 2)), dma((n_wo,)), dma((2,)),
+                dma(()), dma((4,)), dma((n_chip // 2, 2)), dma((n_wo,)), dma((2,)),
                 dma(()), dma(()), dma((2,)), dma((2,)),
-                dma((3, n_chip)), dma((3, n_chip)),
+                dma((4, n_chip)), dma((4, n_chip)),
                 dma((n_chip, 2)), dma((n_chip, 2)),
                 dma((n_chip, 2)), dma((n_chip, 2)),
-                dma((2,)),
             ],
-            compiler_params=pltpu.CompilerParams(collective_id=0, has_side_effects=True, vmem_limit_bytes=62 * 1024 * 1024),
-        )(prompt_blk[0], new_rows, w_q, w_k, w_v, w_o, q_norm_w[None], k_norm_w[None], post_norm_w[None], table)
+            compiler_params=pltpu.CompilerParams(collective_id=0, has_side_effects=True, vmem_limit_bytes=VMEM_MIB * 1024 * 1024),
+        )(keep(prompt_blk[0]), keep(new_rows), w_q, w_k, w_v, w_o, keep(q_norm_w[None]), keep(k_norm_w[None]), keep(post_norm_w[None]), keep(table))
         shape = (seq + 1, heads, HEAD_DIM)
         outs = pl.pallas_call(
             hand_over,
             out_shape=(jax.ShapeDtypeStruct((tok, width), BF16), jax.ShapeDtypeStruct(shape, BF16),
                        jax.ShapeDtypeStruct(shape, BF16), jax.ShapeDtypeStruct((1, width), BF16)),
-            in_specs=[hbm] * 4,
+            in_specs=[vmem] * 4,
             out_specs=(hbm,) * 4,
-            scratch_shapes=[pltpu.VMEM(a.shape, BF16) for a in (outp, kc, vc, outd)] + [dma((2, 4))],
+            scratch_shapes=[dma((4,))],
+            compiler_params=pltpu.CompilerParams(vmem_limit_bytes=8 * 1024 * 1024),
         )(outp, kc, vc, outd)
         return outs[0][None], outs[1][None], outs[2][None], outs[3]
 

time: 69.7 us -> 65.3 us (0.937)
  Pallas kernels: 68.9 us -> 64.5 us
    pallas_call x1, Pallas kernels: 66.6 us -> 63.4 us  [device_step(): pl.pallas_call(functools.partial(kernel, n_dev), out_shape=(jax.ShapeDtyp...]
    pallas_call x1, Pallas kernels: 2.25 us -> 1.18 us  [device_step(): pl.pallas_call(hand_over, out_shape=(jax.ShapeDtypeStruct((tok, width), B...]
where the time goes in v3:
time: 65.3 us; the launch traced here: 65.2 us
  Pallas kernels  64.5 us (99%)
    pallas_call x1, Pallas kernels, device_step(): pl.pallas_call(functools.partial(kernel, n_dev), out_shape=(jax.ShapeDtyp...  63.4 us

profile of v3, /device:TPU:21, one launch (start us, length us, event | category | flops | bytes accessed | tf_op | source)
XLA Modules:
  0.0 65.2 jit_solution(4229040979529268195)
XLA Ops:
  0.6 63.4 %shard_map.129 = (bf16[64,4096]{1,0:T(8,128)(2,1)S(1)}, bf16[2050,128]{1,0:T(8,128)(2,1)S(1)}, bf16[2050,128]{1,0:T(8,128)(2,1)S(1)}, bf16[1,4096]{1,0:T(2,128)(2,1)S(1)}) custom-call(bf16[64,4096]{1,0:T(8,128)(2,1)} %bitcast.7, bf16[1,4096]{1,0:T(2,128)(2,1)} %new_hbm.1, bf16[4096,4096]{1,0:T(8,128)(2,1)} %wq.1, bf16[4096,4096]{1,0:T(8,128)(2,1)} %wk.1, ...), custom_call_target="tpu_custom_call" | custom-call | tf_op jit(solution)/shard_map/pallas_call | solution.py:487
  64.0 1.2 %shard_map.130 = (bf16[64,4096]{1,0:T(8,128)(2,1)}, bf16[1025,2,128]{2,1,0:T(2,128)(2,1)}, bf16[1025,2,128]{2,1,0:T(2,128)(2,1)}, bf16[1,4096]{1,0:T(2,128)(2,1)}) custom-call(bf16[64,4096]{1,0:T(8,128)(2,1)S(1)} %get-tuple-element.12.outp_in, bf16[2050,128]{1,0:T(8,128)(2,1)S(1)} %get-tuple-element.13.kc_in, bf16[2050,128]{1,0:T(8,128)(2,1)S(1)} %get-tuple-element.14.vc_in, ...), custom_call_target="tpu_custom_call" | custom-call | tf_op jit(solution)/shard_map/pallas_call | solution.py:524

commit v4 on v3

--- a/solution.py
+++ b/solution.py
@@ -31,9 +31,9 @@
 
 def kernel(n_dev, x_hbm, new_hbm, wq, wk, wv, wo, qg_hbm, kg_hbm, pg_hbm, tab_hbm,
            outp_ref, kc_ref, vc_ref, outd_ref,
-           new_ref, qg_ref, kg_ref, pg_ref,
+           new_ref, gains,
            xs, pool, tab, raw, ssq, ssq_in, send, recv, new, s_ref, p_ref, vt, osend, orecv, dsend, dsum, acc, stage,
-           xsem, insem, wsem, wosem, tabsem, xs_s, xs_r, ss_s, ss_r, a_s, a_r, d_s, d_r, o_s, o_r):
+           xsem, insem, wsem, wosem, tabsem, xs_s, xs_r, ss_s, ss_r, a_s, a_r, q_r, d_s, d_r, o_s, o_r):
     tok = x_hbm.shape[0]
     width = x_hbm.shape[1]
     rows = 2 * tok
@@ -61,28 +61,32 @@
 
     def w_copy(w_ref, s, half):
         return pltpu.make_async_copy(
-            w_ref.at[:, pl.ds(group_col(2 * s + half), cols)], pool.at[s, :, pl.ds(half * cols, cols)], wsem.at[s, half])
+            w_ref.at[:, pl.ds(group_col(2 * s + half), cols)], pool.at[s, :, pl.ds(half * cols, cols)], wsem.at[s])
+
+    def w_wait(s):
+        pltpu.make_async_copy(pool.at[s], pool.at[s], wsem.at[s]).wait()
 
     def wo_copy(j):
-        return pltpu.make_async_copy(wo.at[:, pl.ds(pl.multiple_of(j * wide, wide), wide)], pool.at[j], wosem.at[j])
+        return pltpu.make_async_copy(wo.at[:, pl.ds(pl.multiple_of(j * wide, wide), wide)], pool.at[j], wosem)
+
+    barrier = pltpu.get_barrier_semaphore()
+    for off in sorted(range(1, n_dev), key=lambda off: -min(off, n_dev - off)):
+        pl.semaphore_signal(barrier, inc=1, device_id={"sp": lax.rem(me + off, n_dev)}, device_id_type=MESH)
 
     my_rows = pl.ds(pl.multiple_of(core * tok, tok), tok)
     x_copy = pltpu.make_async_copy(x_hbm, xs.at[my_rows], xsem)
     x_copy.start()
-    smalls = [pltpu.make_async_copy(a, b, insem.at[n]) for n, (a, b) in enumerate(
-        ((new_hbm, new_ref), (qg_hbm, qg_ref), (kg_hbm, kg_ref), (pg_hbm, pg_ref)))]
+    smalls = [pltpu.make_async_copy(a, b, insem.at[n]) for a, b, n in (
+        (new_hbm, new_ref, 0), (qg_hbm, gains.at[0], 1), (kg_hbm, gains.at[1], 1), (pg_hbm, gains.at[2], 1))]
     w_copy(wv, 0, 0).start()
     w_copy(wv, 0, 1).start()
     for small in smalls:
         small.start()
-    tab_a = pltpu.make_async_copy(tab_hbm.at[pl.ds(pl.multiple_of(chip * rows, rows), rows)], tab.at[pl.ds(0, rows)], tabsem.at[0])
-    tab_b = pltpu.make_async_copy(tab_hbm.at[pl.ds(seq, PAD)], tab.at[pl.ds(rows, PAD)], tabsem.at[1])
+    tab_a = pltpu.make_async_copy(tab_hbm.at[pl.ds(pl.multiple_of(chip * rows, rows), rows)], tab.at[pl.ds(0, rows)], tabsem)
+    tab_b = pltpu.make_async_copy(tab_hbm.at[pl.ds(seq, PAD)], tab.at[pl.ds(rows, PAD)], tabsem)
     tab_a.start()
     tab_b.start()
 
-    barrier = pltpu.get_barrier_semaphore()
-    for off in range(1, n_dev):
-        pl.semaphore_signal(barrier, inc=1, device_id={"sp": lax.rem(me + off, n_dev)}, device_id_type=MESH)
     x_copy.wait()
     for s in range(1, n_step):
         w_copy(wv, s, 0).start()
@@ -93,7 +97,7 @@
     def exchange(t, idx):
         dest = lax.rem(chip + offset_of(idx), n_chip)
         return pltpu.make_async_remote_copy(
-            src_ref=send.at[t, idx], dst_ref=recv.at[t, own_rows], send_sem=a_s.at[t, idx], recv_sem=a_r.at[t, idx],
+            src_ref=send.at[t, idx], dst_ref=recv.at[t, own_rows], send_sem=a_s.at[t], recv_sem=a_r.at[t] if t else q_r.at[idx],
             device_id={"sp": 2 * dest + core}, device_id_type=MESH)
 
     def emit(t, idx, block):
@@ -108,16 +112,15 @@
             new[t] = block[rows:]
 
     def project(s):
-        w_copy(wv, s, 0).wait()
-        w_copy(wv, s, 1).wait()
+        w_wait(s)
         return jnp.dot(xs[...], pool[s], preferred_element_type=F32)
 
-    def half_exchange(idx, which, row):
+    def half_exchange(idx, which):
         dest = lax.rem(chip + offset_of(idx), n_chip)
         at = pl.ds(pl.multiple_of(which * tok, tok), tok)
         return pltpu.make_async_remote_copy(
             src_ref=send.at[2, idx, at], dst_ref=recv.at[2, pl.ds(pl.multiple_of(chip * rows + which * tok, tok), tok)],
-            send_sem=a_s.at[row, idx], recv_sem=a_r.at[row, idx], device_id={"sp": 2 * dest + core}, device_id_type=MESH)
+            send_sem=a_s.at[2], recv_sem=a_r.at[2], device_id={"sp": 2 * dest + core}, device_id_type=MESH)
 
     def half_project(which):
         at = pl.ds(pl.multiple_of(which * tok, tok), tok)
@@ -125,8 +128,7 @@
         for idx in range(2):
             send[2, idx, at, :] = res[:, idx * cols:(idx + 1) * cols]
 
-    w_copy(wv, 0, 0).wait()
-    w_copy(wv, 0, 1).wait()
+    w_wait(0)
     with jax.named_scope("v_first"):
         half_project(core)
     with jax.named_scope("barrier"):
@@ -135,9 +137,9 @@
         src_ref=xs.at[my_rows], dst_ref=xs.at[my_rows], send_sem=xs_s, recv_sem=xs_r, device_id={"sp": sibling}, device_id_type=MESH)
     x_send.start()
     for idx in range(2):
-        half_exchange(idx, core, 3).start()
-    for small in smalls:
-        small.wait()
+        half_exchange(idx, core).start()
+    smalls[0].wait()
+    pltpu.make_async_copy(gains, gains, insem.at[1]).wait()
     xs[pl.ds(rows, PAD), :] = jnp.broadcast_to(new_ref[...], (PAD, width))
     acc[...] = jnp.zeros_like(acc)
     with jax.named_scope("x_arrive"):
@@ -155,11 +157,10 @@
         lax.fori_loop(1, n_step, v_step, 0)
         half_project(1 - core)
         for idx in range(2):
-            half_exchange(idx, 1 - core, 2).start()
+            half_exchange(idx, 1 - core).start()
         w_copy(wk, 0, 0).start()
         w_copy(wk, 0, 1).start()
-    tab_a.wait()
-    tab_b.wait()
+    pltpu.make_async_copy(tab, tab, tabsem).wait()
 
     lane = lax.broadcasted_iota(jnp.int32, (rows + PAD, HEAD_DIM), 1)
     first = lane < HEAD_DIM // 2
@@ -193,7 +194,8 @@
         total = jnp.sum(ssq[t] + ssq_in[t], axis=1, keepdims=True)
         scale = lax.rsqrt(total * (1.0 / width) + NORM_EPS)
 
-        def one(idx, carry):
+        def one(n, carry):
+            idx = n if t else n_chip - 1 - n
             g = g_ref[:, pl.ds(group_col(idx), cols)]
             table = tab[...]
             turned = pltpu.roll(table, HEAD_DIM // 2, 1)
@@ -218,7 +220,7 @@
     with jax.named_scope('k_proj'):
         lax.fori_loop(0, n_step, k_step, 0)
     with jax.named_scope('k_norm'):
-        norm_and_send(1, kg_ref)
+        norm_and_send(1, gains.at[1])
     for j in range(n_step, n_wo):
         wo_copy(j).start()
 
@@ -230,13 +232,13 @@
     with jax.named_scope('q_proj'):
         lax.fori_loop(0, n_step, q_step, 0)
     with jax.named_scope('q_norm'):
-        norm_and_send(0, qg_ref)
-
-    def arrivals(t, start=0):
-        def one(idx, carry):
-            exchange(t, idx).wait_recv()
-            return carry
-        lax.fori_loop(start, n_chip - 1, one, 0)
+        norm_and_send(0, gains.at[0])
+
+    def whole(t):
+        every = pl.ds(0, (n_chip - 1) * rows)
+        return pltpu.make_async_remote_copy(
+            src_ref=recv.at[t, every], dst_ref=recv.at[t, every], send_sem=a_s.at[t], recv_sem=a_r.at[t],
+            device_id={"sp": sibling}, device_id_type=MESH)
 
     def fill_cache(t, cache):
         def one(b, carry):
@@ -252,17 +254,14 @@
         cache[pl.ds(heads * seq, heads), :] = rows_new.astype(BF16)
 
     with jax.named_scope("v_arrive"):
-        for idx in range(2):
-            half_exchange(idx, core, 3).wait_recv()
-            half_exchange(idx, 1 - core, 2).wait_recv()
-        arrivals(2, 2)
+        whole(2).wait_recv()
     with jax.named_scope("v_cache"):
         fill_cache(2, vc_ref)
         for b in range(n_chip):
             for h in range(heads):
                 vt[h, :, b * rows:(b + 1) * rows] = recv[2, b * rows:(b + 1) * rows, h * HEAD_DIM:(h + 1) * HEAD_DIM].astype(F32).T.astype(BF16)
     with jax.named_scope("k_arrive"):
-        arrivals(1)
+        whole(1).wait_recv()
     with jax.named_scope("k_cache"):
         fill_cache(1, kc_ref)
 
@@ -283,28 +282,34 @@
         od = jnp.dot(prob, recv[2, :, at], preferred_element_type=F32) + prob_n * vd.astype(F32)
         dsend[:, at] = od[0:1].astype(BF16).astype(F32)
 
-    def d_copy(off, kk, to):
+    def d_copy(off, to):
         return pltpu.make_async_remote_copy(
-            src_ref=dsend, dst_ref=dsum.at[2 * off + core], send_sem=d_s.at[off, kk], recv_sem=d_r.at[off, core],
+            src_ref=dsend, dst_ref=dsum.at[2 * off + core], send_sem=d_s, recv_sem=d_r,
             device_id={"sp": to}, device_id_type=MESH)
 
-    d_copy(0, 0, sibling).start()
+    d_copy(0, sibling).start()
     for off in range(1, n_chip):
         for kk in range(2):
-            d_copy(off, kk, 2 * lax.rem(chip + off, n_chip) + kk).start()
+            d_copy(off, 2 * lax.rem(chip + off, n_chip) + kk).start()
     dsum[core] = dsend[...]
 
-    def o_copy(i, kk, to, off_o):
+    def d_whole():
+        every = pl.ds(0, n_dev - 1)
+        return pltpu.make_async_remote_copy(
+            src_ref=dsum.at[every], dst_ref=dsum.at[every], send_sem=d_s, recv_sem=d_r,
+            device_id={"sp": sibling}, device_id_type=MESH)
+
+    def o_copy(i, kk, to, off_o, near=0):
         return pltpu.make_async_remote_copy(
             src_ref=osend.at[i, pl.ds(pl.multiple_of(kk * tok, tok), tok)],
             dst_ref=orecv.at[off_o, pl.ds(0, tok), pl.ds(pl.multiple_of(core * cols, cols), cols)],
-            send_sem=o_s.at[i, kk], recv_sem=o_r.at[off_o, core], device_id={"sp": to}, device_id_type=MESH)
+            send_sem=o_s.at[near], recv_sem=o_r.at[off_o], device_id={"sp": to}, device_id_type=MESH)
 
     def fold(block, op):
         return op(block.reshape(block.shape[0] // 8, 8, block.shape[1]), axis=0)
 
     def attend(i):
-        idx = lax.rem(i + n_chip - 1, n_chip)
+        idx = n_chip - 1 - i
         off_q = offset_of(idx)
         src = lax.rem(chip + n_chip - off_q, n_chip)
         off_o = lax.rem(n_chip - off_q, n_chip)
@@ -348,32 +353,30 @@
 
         @pl.when(i == 0)
         def _():
-            o_copy(i, 1 - core, sibling, off_o).start()
+            o_copy(i, 1 - core, sibling, off_o, 1).start()
             orecv[0, pl.ds(0, tok), pl.ds(pl.multiple_of(core * cols, cols), cols)] = osend[0, my_rows, :]
 
     zero_half = jnp.zeros((8, cols), BF16)
 
     def gather(i):
-        off_o = lax.rem(n_chip - offset_of(lax.rem(i + n_chip - 1, n_chip)), n_chip)
+        off_o = lax.rem(n_chip - offset_of(n_chip - 1 - i), n_chip)
         src = lax.rem(chip + n_chip - off_o, n_chip)
 
-        def wait_pair(kk):
+        def arrived(span):
+            at = (off_o, pl.ds(0, tok), span)
             pltpu.make_async_remote_copy(
-                src_ref=osend.at[0, pl.ds(0, tok)], dst_ref=orecv.at[off_o, pl.ds(0, tok), pl.ds(pl.multiple_of(kk * cols, cols), cols)],
-                send_sem=o_s.at[0, 0], recv_sem=o_r.at[off_o, kk], device_id={"sp": sibling}, device_id_type=MESH).wait_recv()
-            pltpu.make_async_remote_copy(
-                src_ref=dsend, dst_ref=dsum.at[2 * off_o + kk], send_sem=d_s.at[0, 0], recv_sem=d_r.at[off_o, kk],
+                src_ref=orecv.at[at], dst_ref=orecv.at[at], send_sem=o_s.at[0], recv_sem=o_r.at[off_o],
                 device_id={"sp": sibling}, device_id_type=MESH).wait_recv()
 
         @pl.when(i == 0)
         def _():
-            wait_pair(1 - core)
+            d_whole().wait_recv()
+            arrived(pl.ds(pl.multiple_of((1 - core) * cols, cols), cols))
 
         @pl.when(i > 0)
         def _():
             with jax.named_scope("o_arrive"):
-                wait_pair(0)
-                wait_pair(1)
+                arrived(pl.ds(0, wide))
 
         d0 = jnp.broadcast_to(dsum[2 * off_o].astype(BF16), (8, cols))
         d1 = jnp.broadcast_to(dsum[2 * off_o + 1].astype(BF16), (8, cols))
@@ -395,23 +398,9 @@
                 src_ref=ssq.at[t], dst_ref=ssq_in.at[t], send_sem=ss_s.at[t], recv_sem=ss_r.at[t],
                 device_id={"sp": sibling}, device_id_type=MESH).wait_send()
 
-        def drain(idx, carry):
-            for t in range(2):
-                exchange(t, idx).wait_send()
-
-            @pl.when(idx >= 2)
-            def _():
-                exchange(2, idx).wait_send()
-
-            for kk in range(2):
-                d_copy(idx + 1, kk, sibling).wait_send()
-            return carry
-
-        lax.fori_loop(0, n_chip - 1, drain, 0)
-        for idx in range(2):
-            half_exchange(idx, core, 3).wait_send()
-            half_exchange(idx, 1 - core, 2).wait_send()
-        d_copy(0, 0, sibling).wait_send()
+        for t in range(3):
+            whole(t).wait_send()
+        d_whole().wait_send()
 
     def both(i, carry):
         @pl.when(i < n_chip)
@@ -421,8 +410,7 @@
 
         @pl.when(i == LAG)
         def _():
-            for j in range(n_wo):
-                wo_copy(j).wait()
+            pltpu.make_async_copy(pool, pool, wosem).wait()
             drain_early()
 
         @pl.when(i >= LAG)
@@ -433,27 +421,25 @@
 
     lax.fori_loop(0, n_chip + LAG, both, 0)
 
-    def finish(r, carry):
-        r_at = pl.ds(pl.multiple_of(r * PAD, PAD), PAD)
+    def finish(r):
+        r_at = pl.ds(r * PAD, PAD)
         val = acc[r_at, :]
         scale = lax.rsqrt(jnp.sum(val * val, axis=1, keepdims=True) * (1.0 / width) + NORM_EPS)
         x_at = pl.ds(pl.multiple_of(core * tok + r * PAD, PAD), PAD)
-        outp_ref[r_at, :] = (xs[x_at, :].astype(F32) + val * scale * pg_ref[...]).astype(BF16)
-        return carry
+        outp_ref[r_at, :] = (xs[x_at, :].astype(F32) + val * scale * gains[2]).astype(BF16)
 
     with jax.named_scope("finish"):
-        lax.fori_loop(0, tok // PAD, finish, 0)
+        for r in range(tok // PAD):
+            finish(r)
         val = acc[pl.ds(tok, 8), :]
         scale = lax.rsqrt(jnp.sum(val * val, axis=1, keepdims=True) * (1.0 / width) + NORM_EPS)
-        outd_ref[...] = (new_ref[...].astype(F32) + (val * scale * pg_ref[...])[0:1]).astype(BF16)
-
-    def drain_o(idx, carry):
-        for kk in range(2):
-            o_copy(idx + 1, kk, sibling, 0).wait_send()
-        return carry
-
-    lax.fori_loop(0, n_chip - 1, drain_o, 0)
-    o_copy(0, 1 - core, sibling, 0).wait_send()
+        outd_ref[...] = (new_ref[...].astype(F32) + (val * scale * gains[2])[0:1]).astype(BF16)
+
+    o_copy(0, 1 - core, sibling, 0, 1).wait_send()
+    far = osend.at[pl.ds(1, n_chip - 1)]
+    pltpu.make_async_remote_copy(
+        src_ref=far, dst_ref=far, send_sem=o_s.at[0], recv_sem=o_r.at[0],
+        device_id={"sp": sibling}, device_id_type=MESH).wait_send()
 
 
 def hand_over(outp_in, kc_in, vc_in, outd_in, outp, kc, vc, outd, sem):
@@ -491,9 +477,7 @@
             out_specs=(vmem,) * 4,
             scratch_shapes=[
                 pltpu.VMEM((1, width), BF16),
-                pltpu.VMEM((1, width), F32),
-                pltpu.VMEM((1, width), F32),
-                pltpu.VMEM((1, width), F32),
+                pltpu.VMEM((3, 1, width), F32),
                 pltpu.VMEM((rows + PAD, width), BF16),
                 pltpu.VMEM((n_wo, width, wide), BF16),
                 pltpu.VMEM((rows + PAD, HEAD_DIM), F32),
@@ -512,11 +496,11 @@
                 pltpu.VMEM((n_dev, 1, cols), F32),
                 pltpu.VMEM((tok + 8, width), F32),
                 pltpu.VMEM((heads * rows, HEAD_DIM), F32),
-                dma(()), dma((4,)), dma((n_chip // 2, 2)), dma((n_wo,)), dma((2,)),
+                dma(()), dma((2,)), dma((n_chip // 2,)), dma(()), dma(()),
                 dma(()), dma(()), dma((2,)), dma((2,)),
-                dma((4, n_chip)), dma((4, n_chip)),
-                dma((n_chip, 2)), dma((n_chip, 2)),
-                dma((n_chip, 2)), dma((n_chip, 2)),
+                dma((3,)), dma((3,)), dma((n_chip,)),
+                dma(()), dma(()),
+                dma((2,)), dma((n_chip,)),
             ],
             compiler_params=pltpu.CompilerParams(collective_id=0, has_side_effects=True, vmem_limit_bytes=VMEM_MIB * 1024 * 1024),
         )(keep(prompt_blk[0]), keep(new_rows), w_q, w_k, w_v, w_o, keep(q_norm_w[None]), keep(k_norm_w[None]), keep(post_norm_w[None]), keep(table))

time: 65.3 us -> 63.1 us (0.966)
  Pallas kernels: 64.5 us -> 62 us
    pallas_call x1, Pallas kernels: 63.4 us -> 60.8 us  [device_step(): pl.pallas_call(functools.partial(kernel, n_dev), out_shape=(jax.ShapeDtyp...]
where the time goes in v4:
time: 63.1 us; the launch traced here: 62.6 us
  Pallas kernels  62 us (98%)
  between operations  0.64 us (1%)
    pallas_call x1, Pallas kernels, device_step(): pl.pallas_call(functools.partial(kernel, n_dev), out_shape=(jax.ShapeDtyp...  60.8 us

profile of v4, /device:TPU:21, one launch (start us, length us, event | category | flops | bytes accessed | tf_op | source)
XLA Modules:
  0.0 62.6 jit_solution(17245411845416823914)
XLA Ops:
  0.6 60.8 %shard_map.129 = (bf16[64,4096]{1,0:T(8,128)(2,1)S(1)}, bf16[2050,128]{1,0:T(8,128)(2,1)S(1)}, bf16[2050,128]{1,0:T(8,128)(2,1)S(1)}, bf16[1,4096]{1,0:T(2,128)(2,1)S(1)}) custom-call(bf16[64,4096]{1,0:T(8,128)(2,1)} %bitcast.7, bf16[1,4096]{1,0:T(2,128)(2,1)} %new_hbm.1, bf16[4096,4096]{1,0:T(8,128)(2,1)} %wq.1, bf16[4096,4096]{1,0:T(8,128)(2,1)} %wk.1, ...), custom_call_target="tpu_custom_call" | custom-call | tf_op jit(solution)/shard_map/pallas_call | solution.py:473
  61.5 1.2 %shard_map.130 = (bf16[64,4096]{1,0:T(8,128)(2,1)}, bf16[1025,2,128]{2,1,0:T(2,128)(2,1)}, bf16[1025,2,128]{2,1,0:T(2,128)(2,1)}, bf16[1,4096]{1,0:T(2,128)(2,1)}) custom-call(bf16[64,4096]{1,0:T(8,128)(2,1)S(1)} %get-tuple-element.12.outp_in, bf16[2050,128]{1,0:T(8,128)(2,1)S(1)} %get-tuple-element.13.kc_in, bf16[2050,128]{1,0:T(8,128)(2,1)S(1)} %get-tuple-element.14.vc_in, ...), custom_call_target="tpu_custom_call" | custom-call | tf_op jit(solution)/shard_map/pallas_call | solution.py:508

commit v5 on v4

--- a/solution.py
+++ b/solution.py
@@ -33,7 +33,7 @@
            outp_ref, kc_ref, vc_ref, outd_ref,
            new_ref, gains,
            xs, pool, tab, raw, ssq, ssq_in, send, recv, new, s_ref, p_ref, vt, osend, orecv, dsend, dsum, acc, stage,
-           xsem, insem, wsem, wosem, tabsem, xs_s, xs_r, ss_s, ss_r, a_s, a_r, q_r, d_s, d_r, o_s, o_r):
+           xsem, insem, wfirst, wsem, wosem, tabsem, xs_s, xs_r, ss_s, ss_r, a_s, a_r, q_r, d_s, d_r, o_s, o_r):
     tok = x_hbm.shape[0]
     width = x_hbm.shape[1]
     rows = 2 * tok
@@ -66,20 +66,28 @@
     def w_wait(s):
         pltpu.make_async_copy(pool.at[s], pool.at[s], wsem.at[s]).wait()
 
+    depth = width // 2
+
+    def w_first(part, half):
+        d_at = pl.ds(part * depth, depth)
+        return pltpu.make_async_copy(
+            wv.at[d_at, pl.ds(group_col(half), cols)], pool.at[0, d_at, pl.ds(half * cols, cols)], wfirst.at[part])
+
     def wo_copy(j):
         return pltpu.make_async_copy(wo.at[:, pl.ds(pl.multiple_of(j * wide, wide), wide)], pool.at[j], wosem)
-
-    barrier = pltpu.get_barrier_semaphore()
-    for off in sorted(range(1, n_dev), key=lambda off: -min(off, n_dev - off)):
-        pl.semaphore_signal(barrier, inc=1, device_id={"sp": lax.rem(me + off, n_dev)}, device_id_type=MESH)
 
     my_rows = pl.ds(pl.multiple_of(core * tok, tok), tok)
     x_copy = pltpu.make_async_copy(x_hbm, xs.at[my_rows], xsem)
     x_copy.start()
     smalls = [pltpu.make_async_copy(a, b, insem.at[n]) for a, b, n in (
         (new_hbm, new_ref, 0), (qg_hbm, gains.at[0], 1), (kg_hbm, gains.at[1], 1), (pg_hbm, gains.at[2], 1))]
-    w_copy(wv, 0, 0).start()
-    w_copy(wv, 0, 1).start()
+    for part in range(2):
+        for half in range(2):
+            w_first(part, half).start()
+    barrier = pltpu.get_barrier_semaphore()
+    for off in sorted(range(1, n_dev), key=lambda off: -min(off, n_dev - off)):
+        pl.semaphore_signal(barrier, inc=1, device_id={"sp": lax.rem(me + off, n_dev)}, device_id_type=MESH)
+
     for small in smalls:
         small.start()
     tab_a = pltpu.make_async_copy(tab_hbm.at[pl.ds(pl.multiple_of(chip * rows, rows), rows)], tab.at[pl.ds(0, rows)], tabsem)
@@ -122,15 +130,22 @@
             src_ref=send.at[2, idx, at], dst_ref=recv.at[2, pl.ds(pl.multiple_of(chip * rows + which * tok, tok), tok)],
             send_sem=a_s.at[2], recv_sem=a_r.at[2], device_id={"sp": 2 * dest + core}, device_id_type=MESH)
 
-    def half_project(which):
+    def half_project(which, res=None):
         at = pl.ds(pl.multiple_of(which * tok, tok), tok)
-        res = jnp.dot(xs[at, :], pool[0], preferred_element_type=F32).astype(BF16)
+        if res is None:
+            res = jnp.dot(xs[at, :], pool[0], preferred_element_type=F32)
+        res = res.astype(BF16)
         for idx in range(2):
             send[2, idx, at, :] = res[:, idx * cols:(idx + 1) * cols]
 
-    w_wait(0)
-    with jax.named_scope("v_first"):
-        half_project(core)
+    res = None
+    for part in range(2):
+        d_at = pl.ds(part * depth, depth)
+        pltpu.make_async_copy(pool.at[0, d_at], pool.at[0, d_at], wfirst.at[part]).wait()
+        with jax.named_scope("v_first"):
+            piece = jnp.dot(xs[my_rows, d_at], pool[0, d_at, :], preferred_element_type=F32)
+            res = piece if res is None else res + piece
+    half_project(core, res)
     with jax.named_scope("barrier"):
         pl.semaphore_wait(barrier, n_dev - 1)
     x_send = pltpu.make_async_remote_copy(
@@ -496,7 +511,7 @@
                 pltpu.VMEM((n_dev, 1, cols), F32),
                 pltpu.VMEM((tok + 8, width), F32),
                 pltpu.VMEM((heads * rows, HEAD_DIM), F32),
-                dma(()), dma((2,)), dma((n_chip // 2,)), dma(()), dma(()),
+                dma(()), dma((2,)), dma((2,)), dma((n_chip // 2,)), dma(()), dma(()),
                 dma(()), dma(()), dma((2,)), dma((2,)),
                 dma((3,)), dma((3,)), dma((n_chip,)),
                 dma(()), dma(()),

time: 63.1 us -> 63.9 us (1.013)
  Pallas kernels: 62 us -> 63.1 us
    pallas_call x1, Pallas kernels: 60.8 us -> 62 us  [device_step(): pl.pallas_call(functools.partial(kernel, n_dev), out_shape=(jax.ShapeDtyp...]
where the time goes in v5:
time: 63.9 us; the launch traced here: 63.8 us
  Pallas kernels  63.1 us (99%)
  between operations  0.64 us (1%)
    pallas_call x1, Pallas kernels, device_step(): pl.pallas_call(functools.partial(kernel, n_dev), out_shape=(jax.ShapeDtyp...  62 us

profile of v5, /device:TPU:21, one launch (start us, length us, event | category | flops | bytes accessed | tf_op | source)
XLA Modules:
  0.0 63.8 jit_solution(14250966668644595817)
XLA Ops:
  0.6 62.0 %shard_map.129 = (bf16[64,4096]{1,0:T(8,128)(2,1)S(1)}, bf16[2050,128]{1,0:T(8,128)(2,1)S(1)}, bf16[2050,128]{1,0:T(8,128)(2,1)S(1)}, bf16[1,4096]{1,0:T(2,128)(2,1)S(1)}) custom-call(bf16[64,4096]{1,0:T(8,128)(2,1)} %bitcast.7, bf16[1,4096]{1,0:T(2,128)(2,1)} %new_hbm.1, bf16[4096,4096]{1,0:T(8,128)(2,1)} %wq.1, bf16[4096,4096]{1,0:T(8,128)(2,1)} %wk.1, ...), custom_call_target="tpu_custom_call" | custom-call | tf_op jit(solution)/shard_map/pallas_call | solution.py:488
  62.6 1.2 %shard_map.130 = (bf16[64,4096]{1,0:T(8,128)(2,1)}, bf16[1025,2,128]{2,1,0:T(2,128)(2,1)}, bf16[1025,2,128]{2,1,0:T(2,128)(2,1)}, bf16[1,4096]{1,0:T(2,128)(2,1)}) custom-call(bf16[64,4096]{1,0:T(8,128)(2,1)S(1)} %get-tuple-element.12.outp_in, bf16[2050,128]{1,0:T(8,128)(2,1)S(1)} %get-tuple-element.13.kc_in, bf16[2050,128]{1,0:T(8,128)(2,1)S(1)} %get-tuple-element.14.vc_in, ...), custom_call_target="tpu_custom_call" | custom-call | tf_op jit(solution)/shard_map/pallas_call | solution.py:523

commit v6 on v4

--- a/solution.py
+++ b/solution.py
@@ -14,7 +14,7 @@
 NORM_EPS = 1e-6
 PAD = 16
 VMEM_MIB = 50
-LAG = 6
+LAG = 8
 MASKED = -1e30
 F32 = jnp.float32
 BF16 = jnp.bfloat16

time: 63.1 us -> 63.2 us (level)
  no operation moved by 1% of the time
where the time goes in v6:
time: 63.2 us; the launch traced here: 62.5 us
  Pallas kernels  61.9 us (98%)
  between operations  0.64 us (1%)
    pallas_call x1, Pallas kernels, device_step(): pl.pallas_call(functools.partial(kernel, n_dev), out_shape=(jax.ShapeDtyp...  60.7 us

profile of v6, /device:TPU:21, one launch (start us, length us, event | category | flops | bytes accessed | tf_op | source)
XLA Modules:
  0.0 62.5 jit_solution(13736895509816179329)
XLA Ops:
  0.6 60.7 %shard_map.129 = (bf16[64,4096]{1,0:T(8,128)(2,1)S(1)}, bf16[2050,128]{1,0:T(8,128)(2,1)S(1)}, bf16[2050,128]{1,0:T(8,128)(2,1)S(1)}, bf16[1,4096]{1,0:T(2,128)(2,1)S(1)}) custom-call(bf16[64,4096]{1,0:T(8,128)(2,1)} %bitcast.7, bf16[1,4096]{1,0:T(2,128)(2,1)} %new_hbm.1, bf16[4096,4096]{1,0:T(8,128)(2,1)} %wq.1, bf16[4096,4096]{1,0:T(8,128)(2,1)} %wk.1, ...), custom_call_target="tpu_custom_call" | custom-call | tf_op jit(solution)/shard_map/pallas_call | solution.py:473
  61.4 1.2 %shard_map.130 = (bf16[64,4096]{1,0:T(8,128)(2,1)}, bf16[1025,2,128]{2,1,0:T(2,128)(2,1)}, bf16[1025,2,128]{2,1,0:T(2,128)(2,1)}, bf16[1,4096]{1,0:T(2,128)(2,1)}) custom-call(bf16[64,4096]{1,0:T(8,128)(2,1)S(1)} %get-tuple-element.12.outp_in, bf16[2050,128]{1,0:T(8,128)(2,1)S(1)} %get-tuple-element.13.kc_in, bf16[2050,128]{1,0:T(8,128)(2,1)S(1)} %get-tuple-element.14.vc_in, ...), custom_call_target="tpu_custom_call" | custom-call | tf_op jit(solution)/shard_map/pallas_call | solution.py:508

commit v7 on v4

--- a/solution.py
+++ b/solution.py
@@ -69,13 +69,14 @@
     def wo_copy(j):
         return pltpu.make_async_copy(wo.at[:, pl.ds(pl.multiple_of(j * wide, wide), wide)], pool.at[j], wosem)
 
+    my_rows = pl.ds(pl.multiple_of(core * tok, tok), tok)
+    x_copy = pltpu.make_async_copy(x_hbm, xs.at[my_rows], xsem)
+    x_copy.start()
+
     barrier = pltpu.get_barrier_semaphore()
     for off in sorted(range(1, n_dev), key=lambda off: -min(off, n_dev - off)):
         pl.semaphore_signal(barrier, inc=1, device_id={"sp": lax.rem(me + off, n_dev)}, device_id_type=MESH)
 
-    my_rows = pl.ds(pl.multiple_of(core * tok, tok), tok)
-    x_copy = pltpu.make_async_copy(x_hbm, xs.at[my_rows], xsem)
-    x_copy.start()
     smalls = [pltpu.make_async_copy(a, b, insem.at[n]) for a, b, n in (
         (new_hbm, new_ref, 0), (qg_hbm, gains.at[0], 1), (kg_hbm, gains.at[1], 1), (pg_hbm, gains.at[2], 1))]
     w_copy(wv, 0, 0).start()

time: 63.1 us -> 64 us (1.014)
  no operation moved by 1% of the time
where the time goes in v7:
time: 64 us; the launch traced here: 63 us
  Pallas kernels  62.4 us (98%)
  between operations  0.64 us (1%)
    pallas_call x1, Pallas kernels, device_step(): pl.pallas_call(functools.partial(kernel, n_dev), out_shape=(jax.ShapeDtyp...  61.2 us

profile of v7, /device:TPU:21, one launch (start us, length us, event | category | flops | bytes accessed | tf_op | source)
XLA Modules:
  0.0 63.0 jit_solution(13701247001950742786)
XLA Ops:
  0.6 61.2 %shard_map.129 = (bf16[64,4096]{1,0:T(8,128)(2,1)S(1)}, bf16[2050,128]{1,0:T(8,128)(2,1)S(1)}, bf16[2050,128]{1,0:T(8,128)(2,1)S(1)}, bf16[1,4096]{1,0:T(2,128)(2,1)S(1)}) custom-call(bf16[64,4096]{1,0:T(8,128)(2,1)} %bitcast.7, bf16[1,4096]{1,0:T(2,128)(2,1)} %new_hbm.1, bf16[4096,4096]{1,0:T(8,128)(2,1)} %wq.1, bf16[4096,4096]{1,0:T(8,128)(2,1)} %wk.1, ...), custom_call_target="tpu_custom_call" | custom-call | tf_op jit(solution)/shard_map/pallas_call | solution.py:474
  61.8 1.2 %shard_map.130 = (bf16[64,4096]{1,0:T(8,128)(2,1)}, bf16[1025,2,128]{2,1,0:T(2,128)(2,1)}, bf16[1025,2,128]{2,1,0:T(2,128)(2,1)}, bf16[1,4096]{1,0:T(2,128)(2,1)}) custom-call(bf16[64,4096]{1,0:T(8,128)(2,1)S(1)} %get-tuple-element.12.outp_in, bf16[2050,128]{1,0:T(8,128)(2,1)S(1)} %get-tuple-element.13.kc_in, bf16[2050,128]{1,0:T(8,128)(2,1)S(1)} %get-tuple-element.14.vc_in, ...), custom_call_target="tpu_custom_call" | custom-call | tf_op jit(solution)/shard_map/pallas_call | solution.py:509
